TPU v7x, 32 devices: a whole 2x2x4 slice. The times are simulated.
32 devices in a mesh: row: 8 (over z, y), col: 4 (over x, core).
Axes of the slice: x: 2, y: 2, z: 4, core: 2. Of those that a mesh axis runs over, the one named last changes fastest.
Arguments:
- grams: bfloat16 [4, 3584, 3584], P(None, 'row', 'col'), as said below
- weights: bfloat16 [4, 3584, 7168], P(None, 'row', 'col'), may hold values from -6 to 6
Outputs:
- merged: float32 [3584, 7168], P('row', 'col')
- residual: float32 [3584, 7168], P('row', 'col')
Inputs may be any that keep to these rules, and one draw needn't show every extreme that they name: `grams`: each of the 4 matrices is symmetric and positive definite.
All inputs are finite; a program needn't handle non-finite values.
Results may differ from a plain program's by a relative error of at most 0.012.
The roundings to bfloat16 on the way count: a program that leaves them out, or rounds other values in their place, can miss the bound.
Values may be sent and summed in bfloat16 or wider, within the bound.
A program may use at most 256 MiB of HBM per device.

v0:
```python
import functools

import jax
import jax.numpy as jnp
from jax import lax
from jax.experimental import pallas as pl
from jax.experimental.pallas import tpu as pltpu
from jax.sharding import PartitionSpec as P

ITERS = 2
STREAMS = 2
MESH = pl.DeviceIdType.MESH


def ring_position(index, n):
    odd = index % 2
    return (1 - odd) * (index // 2) + odd * (n - 1 - index // 2)


def ring_index(position, n):
    back = position // (n // 2)
    return (1 - back) * 2 * position + back * (2 * (n - 1 - position) + 1)


def ring_product_kernel(n, x_ref, high_ref, low_ref, out_ref, ahead, behind, send_a, recv_a, send_b, recv_b):
    me = lax.axis_index("row")
    place = ring_position(me, n)
    right = ring_index((place + 1) % n, n)
    left = ring_index((place + n - 1) % n, n)
    half, columns = ahead.shape[2], x_ref.shape[1]

    barrier = pltpu.get_barrier_semaphore()
    for other in (left, right):
        pl.semaphore_signal(barrier, inc=1, device_id={"row": other}, device_id_type=MESH)
    pl.semaphore_wait(barrier, 2)

    def send(source, held, slot, sends, recvs, target):
        return pltpu.make_async_remote_copy(
            src_ref=source,
            dst_ref=held.at[slot],
            send_sem=sends.at[slot],
            recv_sem=recvs.at[slot],
            device_id={"row": target},
            device_id_type=MESH,
        )

    def add(where, owner, block):
        out_ref[:, where] += jnp.dot(high_ref[owner], block, preferred_element_type=jnp.float32) + jnp.dot(
            low_ref[owner], block, preferred_element_type=jnp.float32
        )

    front, rest = slice(0, half), slice(half, columns)
    send(x_ref.at[:, pl.ds(0, half)], ahead, 0, send_a, recv_a, right).start()
    send(x_ref.at[:, pl.ds(half, columns - half)], behind, 0, send_b, recv_b, left).start()
    out_ref[...] = jnp.zeros_like(out_ref)
    add(front, me, x_ref[:, front])
    add(rest, me, x_ref[:, rest])

    def step(s, carry):
        send(ahead.at[s], ahead, s, send_a, recv_a, right).wait()
        send(behind.at[s], behind, s, send_b, recv_b, left).wait()

        @pl.when(s < n - 2)
        def _():
            send(ahead.at[s], ahead, s + 1, send_a, recv_a, right).start()
            send(behind.at[s], behind, s + 1, send_b, recv_b, left).start()

        add(front, ring_index((place + n - 1 - s) % n, n), ahead[s])
        add(rest, ring_index((place + 1 + s) % n, n), behind[s])
        return carry

    lax.fori_loop(0, n - 1, step, 0)


def ring_product(n, rounded, high, low):
    rows, columns = rounded.shape
    half = pl.cdiv(columns, 256) * 128
    held = [pltpu.VMEM((n - 1, rows, size), jnp.bfloat16) for size in (half, columns - half)]
    return pl.pallas_call(
        functools.partial(ring_product_kernel, n),
        out_shape=jax.ShapeDtypeStruct((rows, columns), jnp.float32),
        in_specs=[pl.BlockSpec(memory_space=pltpu.VMEM)] * 3,
        out_specs=pl.BlockSpec(memory_space=pltpu.VMEM),
        scratch_shapes=held + [pltpu.SemaphoreType.DMA((n - 1,))] * 4,
        compiler_params=pltpu.CompilerParams(collective_id=1, has_side_effects=True, vmem_limit_bytes=48 * 2**20),
    )(rounded, high, low)


def row_sum_kernel(n, x_ref, out_ref, held, sends, recvs):
    me = lax.axis_index("row")
    barrier = pltpu.get_barrier_semaphore()
    for k in range(1, n):
        pl.semaphore_signal(barrier, inc=1, device_id={"row": (me + k) % n}, device_id_type=MESH)
    pl.semaphore_wait(barrier, n - 1)
    copies = []
    for k in range(1, n):
        copy = pltpu.make_async_remote_copy(
            src_ref=x_ref,
            dst_ref=held.at[k - 1],
            send_sem=sends.at[k - 1],
            recv_sem=recvs.at[k - 1],
            device_id={"row": (me + k) % n},
            device_id_type=MESH,
        )
        copy.start()
        copies.append(copy)
    for copy in copies:
        copy.wait()
    total = x_ref[...]
    for k in range(n - 1):
        total = total + held[k]
    out_ref[...] = total


def row_sum(n, values):
    flat = values.reshape(-1, 128)
    return pl.pallas_call(
        functools.partial(row_sum_kernel, n),
        out_shape=jax.ShapeDtypeStruct(flat.shape, jnp.float32),
        in_specs=[pl.BlockSpec(memory_space=pltpu.VMEM)],
        out_specs=pl.BlockSpec(memory_space=pltpu.VMEM),
        scratch_shapes=[pltpu.VMEM((n - 1,) + flat.shape, jnp.float32)] + [pltpu.SemaphoreType.DMA((n - 1,))] * 2,
        compiler_params=pltpu.CompilerParams(collective_id=2, has_side_effects=True),
    )(flat).reshape(values.shape)


def shards(row_count, grams, weights):
    models, slab_rows, slab_cols = grams.shape
    col_count = weights.shape[2]
    row_index = lax.axis_index("row")
    first_row = row_index * slab_rows
    width = col_count // STREAMS

    gathered = lax.all_gather(grams, "col", axis=0)
    parts = gathered.shape[0]

    def own_columns(array):
        per_slab = slab_cols // slab_rows
        slab = lax.dynamic_index_in_dim(array, row_index // per_slab, 0, keepdims=False)
        offset = (row_index % per_slab) * slab_rows
        return lax.dynamic_slice_in_dim(slab, offset, slab_rows, slab.ndim - 1)

    block = own_columns(gathered)
    on_diag = jnp.arange(slab_rows)[:, None] == jnp.arange(slab_rows)[None, :]
    diags = jnp.sum(jnp.where(on_diag, block.astype(jnp.float32), 0.0), axis=2)
    total_diag = jnp.sum(diags, axis=0)
    total = jnp.sum(gathered.astype(jnp.float32), axis=1)
    total = total.reshape(parts, slab_rows, -1, slab_rows).swapaxes(1, 2).reshape(row_count, slab_rows, slab_rows)
    high = total.astype(jnp.bfloat16)
    low = (total - high.astype(jnp.float32)).astype(jnp.bfloat16)
    first_part = (((0,), (0,)), ((), ()))
    depth = models * slab_rows
    flat = gathered.reshape(parts, depth, slab_cols)
    flat_block = block.reshape(depth, slab_rows)
    in_block = (jnp.arange(parts * slab_cols) // slab_rows) == row_index

    def right_side(weight):
        flat_weight = weight.reshape(depth, width)
        pieces = []
        for d in range(parts):
            piece = lax.dot_general(flat[d], flat_weight, first_part, preferred_element_type=jnp.float32)
            keep = in_block[d * slab_cols : (d + 1) * slab_cols]
            pieces.append(jnp.where(keep[:, None], 0.0, piece).astype(jnp.bfloat16))
        others = lax.psum_scatter(jnp.concatenate(pieces, axis=0), "row", scatter_dimension=0, tiled=True)
        own = lax.dot_general(flat_block, flat_weight, first_part, preferred_element_type=jnp.float32)
        diag_term = jnp.sum(diags[:, :, None] * weight.astype(jnp.float32), axis=0)
        return 0.9 * (own + others.astype(jnp.float32)) + 0.1 * diag_term

    def column_sum(values):
        return row_sum(row_count, jnp.sum(values, axis=0))

    starts = [right_side(lax.slice_in_dim(weights, s * width, (s + 1) * width, axis=2)) for s in range(STREAMS)]
    residual = jnp.concatenate(starts, axis=1)
    direction = residual
    merged = jnp.zeros_like(residual)
    norm_now = column_sum(residual * residual)
    for iteration in range(ITERS):
        rounded = direction.astype(jnp.bfloat16)
        product = ring_product(row_count, rounded, high, low)
        mapped = 0.9 * product + 0.1 * total_diag[:, None] * rounded.astype(jnp.float32)
        curvature = column_sum(direction * mapped)
        step_length = norm_now / curvature
        merged = merged + step_length * direction
        residual = residual - step_length * mapped
        if iteration + 1 < ITERS:
            norm_next = column_sum(residual * residual)
            direction = residual + norm_next / norm_now * direction
            norm_now = norm_next
    return merged, residual


def solution(mesh):
    placed = (P(None, "row", "col"), P(None, "row", "col"))
    return jax.shard_map(
        functools.partial(shards, mesh.shape["row"]),
        mesh=mesh,
        in_specs=placed,
        out_specs=(P("row", "col"), P("row", "col")),
        check_vma=False,
    )
```

profile of v0, /device:TPU:28, one launch (start us, length us, event | category | flops | bytes accessed | tf_op | source)
XLA Modules:
  0.0 689.2 jit_solution(2484154185009685751)
XLA Ops:
  8.0 5.1 fusion.10
  13.1 81.0 %all-gather.3.cloned.1.call-done = bf16[16,448,896]{2,1,0:T(8,128)(2,1)} async-done(((bf16[4,448,896]{2,1,0:T(8,128)(2,1)}), bf16[16,448,896]{2,1,0:T(8,128)(2,1)}) %all-gather.3.cloned.1.call-update) | async-done | bytes 12845072 | tf_op jit(solution)/shard_map/all_gather | solution.py:134
  94.1 5.7 fusion.8
  99.9 5.2 select_convert_fusion
  105.0 4.6 select_convert_fusion.1
  109.6 4.6 select_convert_fusion.2
  114.3 4.6 select_convert_fusion.3
  118.9 6.0 pad_maximum_fusion.2
  125.2 6.7 select_convert_fusion.4
  131.9 4.6 select_convert_fusion.5
  136.5 4.7 select_convert_fusion.6
  141.2 4.6 select_convert_fusion.7
  145.8 6.1 pad_maximum_fusion.1
  155.7 10.5 %convert_reduce_fusion = f32[4,448,896]{2,1,0:T(8,128)S(1)} fusion(bf16[16,448,896]{2,1,0:T(8,128)(2,1)} %all-gather.3.cloned.1.call-done), kind=kLoop, calls=%fused_computation | loop fusion | flops 11239424 | bytes 19267584 | tf_op jit(solution)/shard_map/reduce_sum | solution.py:147
  180.5 62.9 %reduce-scatter.5.cloned.1.call-done = bf16[448,896]{1,0:T(8,128)(2,1)} async-done(((bf16[3584,896]{1,0:T(8,128)(2,1)}), bf16[448,896]{1,0:T(8,128)(2,1)}) %reduce-scatter.5.cloned.1.call-update) | async-done | bytes 802832 | tf_op jit(solution)/shard_map/reduce_scatter | solution.py:164
  247.9 118.2 %reduce-scatter.3.cloned.1.call-done = bf16[448,896]{1,0:T(8,128)(2,1)} async-done(((bf16[3584,896]{1,0:T(8,128)(2,1)}), bf16[448,896]{1,0:T(8,128)(2,1)}) %reduce-scatter.3.cloned.1.call-update) | async-done | bytes 802832 | tf_op jit(solution)/shard_map/reduce_scatter | solution.py:164
  366.1 4.5 multiply_add_fusion.5
  370.8 130.7 %shard_map.42 = f32[448,1792]{1,0:T(8,128)S(1)} custom-call(bf16[448,1792]{1,0:T(8,128)(2,1)S(1)} %fusion.7.x_ref, bf16[8,448,448]{2,1,0:T(8,128)(2,1)} %get-tuple-element.9.high_ref, bf16[8,448,448]{2,1,0:T(8,128)(2,1)} %get-tuple-element.8.low_ref), custom_call_target="tpu_custom_call" | custom-call | tf_op jit(solution)/shard_map/pallas_call | solution.py:79
  503.0 8.2 %shard_map.43 = f32[14,128]{1,0:T(8,128)} custom-call(f32[14,128]{1,0:T(8,128)} %bitcast.69), custom_call_target="tpu_custom_call" | custom-call | tf_op jit(solution)/shard_map/pallas_call | solution.py:117
  511.2 8.1 %shard_map.41 = f32[14,128]{1,0:T(8,128)} custom-call(f32[14,128]{1,0:T(8,128)} %bitcast.68), custom_call_target="tpu_custom_call" | custom-call | tf_op jit(solution)/shard_map/pallas_call | solution.py:117
  523.4 8.1 %shard_map.44 = f32[14,128]{1,0:T(8,128)} custom-call(f32[14,128]{1,0:T(8,128)} %bitcast.70), custom_call_target="tpu_custom_call" | custom-call | tf_op jit(solution)/shard_map/pallas_call | solution.py:117
  535.2 130.5 %shard_map.45 = f32[448,1792]{1,0:T(8,128)S(1)} custom-call(bf16[448,1792]{1,0:T(8,128)(2,1)S(1)} %fusion.2.x_ref, bf16[8,448,448]{2,1,0:T(8,128)(2,1)} %get-tuple-element.9.high_ref, bf16[8,448,448]{2,1,0:T(8,128)(2,1)} %get-tuple-element.8.low_ref), custom_call_target="tpu_custom_call" | custom-call | tf_op jit(solution)/shard_map/pallas_call | solution.py:79
  667.9 8.2 %shard_map.46 = f32[14,128]{1,0:T(8,128)} custom-call(f32[14,128]{1,0:T(8,128)} %bitcast.71), custom_call_target="tpu_custom_call" | custom-call | tf_op jit(solution)/shard_map/pallas_call | solution.py:117
  676.8 5.5 multiply_subtract_fusion
  (63 shorter events, 35.5 us)
Async XLA Ops:
  7.2 86.9 %all-gather.3.cloned.1.call-start = ((), (), s32[]{:S(2)}) async-start(), calls=%async_computation.4 | async-start | bytes 16056320 | tf_op jit(solution)/shard_map/all_gather | solution.py:134
  7.9 235.5 %reduce-scatter.5.cloned.1.call-start = ((), (), s32[]{:S(2)}) async-start(), calls=%async_computation.3 | async-start | bytes 7225344 | tf_op jit(solution)/shard_map/reduce_scatter | solution.py:164
  13.1 128.1 %copy-start.6 = (bf16[4,448,896]{2,1,0:T(8,128)(2,1)}, bf16[4,448,896]{2,1,0:T(8,128)(2,1)S(1)}, u32[]{:S(2)}) copy-start(bf16[4,448,896]{2,1,0:T(8,128)(2,1)S(1)} %get-tuple-element.19) | copy-start | bytes 9633796
  94.1 5.8 copy-start.7
  99.8 5.2 copy-start.12
  99.8 9.8 %copy-start.14 = (bf16[4,448,896]{2,1,0:T(8,128)(2,1)}, bf16[4,448,896]{2,1,0:T(8,128)(2,1)S(1)}, u32[]{:S(2)}) copy-start(bf16[4,448,896]{2,1,0:T(8,128)(2,1)S(1)} %get-tuple-element.12) | copy-start | bytes 9633796
  99.8 9.8 %copy-start.10 = (bf16[4,448,896]{2,1,0:T(8,128)(2,1)}, bf16[4,448,896]{2,1,0:T(8,128)(2,1)S(1)}, u32[]{:S(2)}) copy-start(bf16[4,448,896]{2,1,0:T(8,128)(2,1)S(1)} %get-tuple-element.14) | copy-start | bytes 9633796
  99.8 14.4 %copy-start.8 = (bf16[4,448,896]{2,1,0:T(8,128)(2,1)}, bf16[4,448,896]{2,1,0:T(8,128)(2,1)S(1)}, u32[]{:S(2)}) copy-start(bf16[4,448,896]{2,1,0:T(8,128)(2,1)S(1)} %get-tuple-element.11) | copy-start | bytes 9633796
  124.9 241.2 %reduce-scatter.3.cloned.1.call-start = ((), (), s32[]{:S(2)}) async-start(), calls=%async_computation.2 | async-start | bytes 7225344 | tf_op jit(solution)/shard_map/reduce_scatter | solution.py:164
  125.2 6.7 copy-start.13
  131.9 4.6 copy-start.11
  136.5 4.7 copy-start.9
  166.2 6.3 slice-start
  169.5 3.1 slice-start.1
  247.9 122.8 %copy-start.1 = (f32[448,896]{1,0:T(8,128)}, f32[448,896]{1,0:T(8,128)S(1)}, u32[]{:S(2)}) copy-start(f32[448,896]{1,0:T(8,128)S(1)} %multiply_add_fusion.4) | copy-start | bytes 4816900
  370.7 130.9 %copy-start.4 = (f32[448,896]{1,0:T(8,128)}, f32[448,896]{1,0:T(8,128)S(1)}, u32[]{:S(2)}) copy-start(f32[448,896]{1,0:T(8,128)S(1)} %multiply_add_fusion.5) | copy-start | bytes 4816900
  370.8 130.8 %copy-start.2 = (f32[448,896]{1,0:T(8,128)S(1)}, f32[448,896]{1,0:T(8,128)}, u32[]{:S(2)}) copy-start(f32[448,896]{1,0:T(8,128)} %copy-done.1) | copy-start | bytes 4816900
  520.1 11.5 %copy-start.16 = (f32[14,128]{1,0:T(8,128)S(1)}, f32[14,128]{1,0:T(8,128)}, u32[]{:S(2)}) copy-start(f32[14,128]{1,0:T(8,128)} %shard_map.41) | copy-start | bytes 21508
  535.1 130.6 %copy-start.3 = (f32[448,896]{1,0:T(8,128)S(1)}, f32[448,896]{1,0:T(8,128)}, u32[]{:S(2)}) copy-start(f32[448,896]{1,0:T(8,128)} %copy-done.1) | copy-start | bytes 4816900
  535.2 130.6 %copy-start.5 = (f32[448,896]{1,0:T(8,128)S(1)}, f32[448,896]{1,0:T(8,128)}, u32[]{:S(2)}) copy-start(f32[448,896]{1,0:T(8,128)} %copy-done.4) | copy-start | bytes 4816900
  665.7 2.2 copy-start
  665.8 10.3 %copy-start.15 = (f32[14,128]{1,0:T(8,128)S(1)}, f32[14,128]{1,0:T(8,128)}, u32[]{:S(2)}) copy-start(f32[14,128]{1,0:T(8,128)} %shard_map.44) | copy-start | bytes 21508
Sparse Core Ops, SparseCore 0:
  9.5 84.4 all-gather.2
  125.1 118.2 reduce-scatter.4
  246.9 119.1 reduce-scatter.2
where the time goes:
time: 699 us; the launch traced here: 689 us
  Pallas kernels  294 us (42%)
  waiting for transfers between devices  263 us (38%)
  other arithmetic  54.8 us (8%)
  matrix products  48.7 us (7%)
  between operations  14.6 us (2%)
  local copies, waits for them, and re-layouts  14.2 us (2%)
    pallas_call x2, Pallas kernels, ring_product(): pl.pallas_call(functools.partial(ring_product_kernel, n), out_shape=jax.S...  261 us
    reduce_scatter x2, waiting for transfers between devices, right_side(): lax.psum_scatter(jnp.concatenate(pieces, axis=0), 'row', scatter_dimensio...  181 us
    all_gather x1, waiting for transfers between devices, shards(): gathered = lax.all_gather(grams, 'col', axis=0)  81 us
    dot_general x8, matrix products, right_side(): lax.dot_general(flat[d], flat_weight, first_part, preferred_element_type=...  39.7 us
    pallas_call x4, Pallas kernels, row_sum(): pl.pallas_call(functools.partial(row_sum_kernel, n), out_shape=jax.ShapeD...  32.6 us
  transfers between devices with their start and end apart: 3, of which 3 were waited for; matrix products, arithmetic and copies ran while one was open for 9% of the time, Pallas kernels for 0%

commit v1 on v0

v1 whole, which is shorter than its diff:
```python
import functools

import jax
import jax.numpy as jnp
from jax import lax
from jax.experimental import pallas as pl
from jax.experimental.pallas import tpu as pltpu
from jax.sharding import PartitionSpec as P

ITERS = 2
STREAMS = 2
MESH = pl.DeviceIdType.MESH
VMEM_BYTES = 63 * 2**20


def ring_position(index, n):
    odd = index % 2
    return (1 - odd) * (index // 2) + odd * (n - 1 - index // 2)


def ring_index(position, n):
    back = position // (n // 2)
    return (1 - back) * 2 * position + back * (2 * (n - 1 - position) + 1)


def remote(source, target, send, recv, where):
    return pltpu.make_async_remote_copy(
        src_ref=source, dst_ref=target, send_sem=send, recv_sem=recv, device_id=where, device_id_type=MESH
    )


def row_gather_kernel(n, x_ref, d_ref, out_ref, dout_ref, send_a, recv_a, send_b, recv_b):
    me = lax.axis_index("row")
    place = ring_position(me, n)
    right = {"row": ring_index((place + 1) % n, n)}
    left = {"row": ring_index((place + n - 1) % n, n)}
    rows = x_ref.shape[0]
    cut = rows // 32 * 16
    hops = n // 2

    barrier = pltpu.get_barrier_semaphore()
    for other in (left, right):
        pl.semaphore_signal(barrier, inc=1, device_id=other, device_id_type=MESH)
    pl.semaphore_wait(barrier, 2)

    def pair(hop, window):
        ahead = ring_index((place + n - hop) % n, n)
        behind = ring_index((place + hop) % n, n)
        first, second = window
        out = []
        for slot, (held, wa, wb) in enumerate(((out_ref, first, second), (dout_ref, None, None))):
            a = held.at[ahead] if wa is None else held.at[ahead, wa, :]
            b = held.at[behind] if wb is None else held.at[behind, wb, :]
            out.append(remote(a, a, send_a.at[slot, hop], recv_a.at[slot, hop], right))
            out.append(remote(b, b, send_b.at[slot, hop], recv_b.at[slot, hop], left))
        return out

    out_ref[me] = x_ref[...]
    dout_ref[me] = d_ref[...]
    whole = (pl.ds(0, rows), pl.ds(0, rows))
    last = (pl.ds(0, cut), pl.ds(cut, rows - cut))
    for hop in range(hops):
        copies = pair(hop, last if hop == hops - 1 else whole)
        if hop == hops - 1:
            copies = copies[:3]
        for copy in copies:
            copy.start()
        for copy in copies:
            copy.wait()


def row_gather(n, slab, diag):
    shape = jax.ShapeDtypeStruct((n,) + slab.shape, slab.dtype)
    dshape = jax.ShapeDtypeStruct((n,) + diag.shape, diag.dtype)
    vmem = pl.BlockSpec(memory_space=pltpu.VMEM)
    return pl.pallas_call(
        functools.partial(row_gather_kernel, n),
        out_shape=(shape, dshape),
        in_specs=[vmem] * 2,
        out_specs=(vmem, vmem),
        scratch_shapes=[pltpu.SemaphoreType.DMA((2, n // 2))] * 4,
        compiler_params=pltpu.CompilerParams(collective_id=1, has_side_effects=True, vmem_limit_bytes=VMEM_BYTES),
        cost_estimate=pl.CostEstimate(flops=0, bytes_accessed=200 * 2**20, transcendentals=0),
    )(slab, diag)


def col_gather_kernel(parts, pieces, x_ref, d_ref, out_ref, dout_ref, own, copied, send, recv, dsend, drecv):
    me = lax.axis_index("col")
    chips = parts // 2
    chip, core = me // 2, me % 2
    twin = {"col": chip * 2 + 1 - core}
    rows = x_ref.shape[0] // pieces
    barrier = pltpu.get_barrier_semaphore()
    for k in range(1, parts):
        pl.semaphore_signal(barrier, inc=1, device_id={"col": (me + k) % parts}, device_id_type=MESH)
    pl.semaphore_wait(barrier, parts - 1)

    def peer(k):
        return {"col": (chip + k) % chips * 2 + core}

    def window(piece):
        return pl.ds(piece * rows, rows)

    started = []
    for piece in range(pieces):
        for k in list(range(1, chips)) + [0]:
            copy = remote(
                x_ref.at[window(piece), :],
                out_ref.at[me, window(piece), :],
                send.at[k, piece],
                recv.at[k, piece],
                peer(k) if k else twin,
            )
            copy.start()
            started.append(copy)
    dcopies = []
    dout_ref[me] = d_ref[...]
    for k in range(1, parts):
        copy = remote(d_ref, dout_ref.at[me], dsend.at[k], drecv.at[k], {"col": (me + k) % parts})
        copy.start()
        dcopies.append(copy)
    mine = pltpu.make_async_copy(x_ref, out_ref.at[me], own)
    mine.start()
    forwards = []
    for piece in range(pieces):
        for k in range(1, chips):
            origin = (chip + chips - k) % chips * 2 + core
            part = out_ref.at[origin, window(piece), :]
            remote(part, part, send.at[k, piece], recv.at[k, piece], twin).wait_recv()
            copy = remote(part, part, send.at[chips + k - 1, piece], recv.at[chips + k - 1, piece], twin)
            copy.start()
            forwards.append(copy)
    for piece in range(pieces):
        for k in range(chips):
            copy = started[piece * chips + (k - 1) % chips]
            copy.wait_send()
            if k == 0:
                copy.wait_recv()
    for copy in forwards + dcopies:
        copy.wait()
    mine.wait()


def col_gather(parts, slabs, diags):
    pieces = 4
    any_space = pl.BlockSpec(memory_space=pl.ANY)
    vmem = pl.BlockSpec(memory_space=pltpu.VMEM)
    sems = pltpu.SemaphoreType.DMA((parts, pieces))
    return pl.pallas_call(
        functools.partial(col_gather_kernel, parts, pieces),
        out_shape=(
            jax.ShapeDtypeStruct((parts,) + slabs.shape, slabs.dtype),
            jax.ShapeDtypeStruct((parts,) + diags.shape, diags.dtype),
        ),
        in_specs=[vmem] * 2,
        out_specs=(any_space, vmem),
        scratch_shapes=[
            pltpu.SemaphoreType.DMA,
            pltpu.SemaphoreType.DMA,
            sems,
            sems,
            pltpu.SemaphoreType.DMA((parts,)),
            pltpu.SemaphoreType.DMA((parts,)),
        ],
        compiler_params=pltpu.CompilerParams(collective_id=2, has_side_effects=True, vmem_limit_bytes=24 * 2**20),
        cost_estimate=pl.CostEstimate(flops=0, bytes_accessed=400 * 2**20, transcendentals=0),
    )(slabs, diags)


def solve_kernel(
    n, parts, hi_ref, lo_ref, t_ref, d_ref, om_ref, or_ref,
    tv, v, lo, direction, residual, mapped, out_m, out_r, t_sem, send, recv,
):
    me = lax.axis_index("row")
    rows, q = hi_ref.shape[1], hi_ref.shape[2]
    depth = tv.shape[2]
    f32 = jnp.float32

    barrier = pltpu.get_barrier_semaphore()
    for k in range(1, n):
        pl.semaphore_signal(barrier, inc=1, device_id={"row": (me + k) % n}, device_id_type=MESH)
    loads = [pltpu.make_async_copy(t_ref.at[c], tv.at[c], t_sem.at[c]) for c in range(parts)]
    for load in loads:
        load.start()
    pl.semaphore_wait(barrier, n - 1)

    def block(i):
        return pl.ds(pl.multiple_of(i * rows, 16), rows)

    def moved(kind, k, source, target):
        other = (me + k) % n
        return remote(source(other), target, send.at[kind, k], recv.at[kind, k], {"row": other})

    incoming = [
        [moved(0, k, lambda i: hi_ref.at[i], v.at[block(me), :]) for k in range(1, n)],
        [moved(1, k, lambda i: lo_ref.at[i], lo.at[block(me), :]) for k in range(1, n)],
    ]
    for group in incoming:
        for copy in group:
            copy.start()
    v[block(me), :] = hi_ref[me]
    lo[block(me), :] = lo_ref[me]

    def product(_):
        def step(i, carry):
            here = block(i)
            total = jnp.zeros((rows, q), f32)
            for c in range(parts):
                total += jnp.dot(tv[c, here, :], v[pl.ds(c * depth, depth), :], preferred_element_type=f32)
            mapped[here, :] = 0.9 * total + d_ref[here, :] * v[here, :].astype(f32)
            return carry

        lax.fori_loop(0, n, step, 0)

    def column_sum(terms):
        def step(i, total):
            return total + jnp.sum(terms(block(i)), axis=0, keepdims=True)

        return lax.fori_loop(0, n, step, jnp.zeros((1, q), f32))

    for copy in incoming[0]:
        copy.wait()
    for load in loads:
        load.wait()
    product(0)
    for copy in incoming[1]:
        copy.wait()

    def first(here):
        start = v[here, :].astype(f32) + lo[here, :].astype(f32)
        direction[here, :] = start
        return start * start

    norm = column_sum(first)
    curvature = column_sum(lambda here: direction[here, :] * mapped[here, :])
    step_a = norm / curvature

    def second(here):
        left = direction[here, :] - step_a * mapped[here, :]
        residual[here, :] = left
        return left * left

    norm_next = column_sum(second)
    scale = norm_next / norm

    def turn(i, carry):
        here = block(i)
        v[here, :] = (residual[here, :] + scale * direction[here, :]).astype(jnp.bfloat16)
        return carry

    lax.fori_loop(0, n, turn, 0)
    product(0)
    curvature = column_sum(lambda here: (residual[here, :] + scale * direction[here, :]) * mapped[here, :])
    step_b = norm_next / curvature

    def leaving(k):
        i = (me + k) % n
        return [
            remote(held.at[block(i), :], target.at[me], send.at[kind, k], recv.at[kind, k], {"row": i})
            for kind, held, target in ((2, out_m, om_ref), (3, out_r, or_ref))
        ]

    def outputs(i):
        here = block(i)
        left, start = residual[here, :], direction[here, :]
        merged = step_a * start + step_b * (left + scale * start)
        return merged.astype(jnp.bfloat16), (left - step_b * mapped[here, :]).astype(jnp.bfloat16)

    def finish(k, carry):
        i = (me + k) % n
        here = block(i)
        out_m[here, :], out_r[here, :] = outputs(i)

        @pl.when(k > 1)
        def _():
            for copy in leaving(k - 1):
                copy.start()

        return carry

    lax.fori_loop(1, n, finish, 0)
    om_ref[me], or_ref[me] = outputs(me)
    for copy in leaving(n - 1):
        copy.start()

    def drain(k, carry):
        for copy in leaving(k):
            copy.wait()
        return carry

    lax.fori_loop(1, n, drain, 0)


def solve(n, high, low, total, diag):
    parts = total.shape[0]
    _, rows, q = high.shape
    vmem = pl.BlockSpec(memory_space=pltpu.VMEM)
    half, full = pltpu.VMEM((n * rows, q), jnp.bfloat16), pltpu.VMEM((n * rows, q), jnp.float32)
    out = jax.ShapeDtypeStruct((n, rows, q), jnp.bfloat16)
    return pl.pallas_call(
        functools.partial(solve_kernel, n, parts),
        out_shape=(out, out),
        in_specs=[vmem, vmem, pl.BlockSpec(memory_space=pl.ANY), vmem],
        out_specs=(vmem, vmem),
        scratch_shapes=[
            pltpu.VMEM(total.shape, jnp.bfloat16),
            half,
            half,
            full,
            full,
            full,
            half,
            half,
            pltpu.SemaphoreType.DMA((parts,)),
            pltpu.SemaphoreType.DMA((4, n)),
            pltpu.SemaphoreType.DMA((4, n)),
        ],
        compiler_params=pltpu.CompilerParams(collective_id=3, has_side_effects=True, vmem_limit_bytes=VMEM_BYTES),
    )(high, low, total, diag)


def shards(row_count, col_parts, grams, weights):
    models, slab_rows, slab_cols = grams.shape
    col_count = weights.shape[2]
    row_index = lax.axis_index("row")
    width = col_count // STREAMS

    own_total = jnp.sum(grams.astype(jnp.float32), axis=0)
    row_ids = row_index * slab_rows + jnp.arange(slab_rows)[:, None]
    col_ids = lax.axis_index("col") * slab_cols + jnp.arange(slab_cols)[None, :]
    diagonal = row_ids == col_ids
    slab = jnp.where(diagonal, 0.0, own_total).astype(jnp.bfloat16)
    own_diag = jnp.sum(jnp.where(diagonal, own_total, 0.0), axis=1)
    padded = -(-slab_rows // 1024) * 1024
    own_diag = jnp.pad(own_diag, (0, padded - slab_rows)).reshape(-1, 128)
    slabs, some_diags = row_gather(row_count, slab, own_diag)

    gathered = lax.all_gather(grams, "col", axis=0)
    parts = gathered.shape[0]

    def own_columns(array):
        per_slab = slab_cols // slab_rows
        piece = lax.dynamic_index_in_dim(array, row_index // per_slab, 0, keepdims=False)
        offset = (row_index % per_slab) * slab_rows
        return lax.dynamic_slice_in_dim(piece, offset, slab_rows, piece.ndim - 1)

    block = own_columns(gathered)
    on_diag = jnp.arange(slab_rows)[:, None] == jnp.arange(slab_rows)[None, :]
    diags = jnp.sum(jnp.where(on_diag, block.astype(jnp.float32), 0.0), axis=2)
    first_part = (((0,), (0,)), ((), ()))
    depth = models * slab_rows
    flat = gathered.reshape(parts, depth, slab_cols)
    flat_block = block.reshape(depth, slab_rows)
    in_block = (jnp.arange(parts * slab_cols) // slab_rows) == row_index

    def right_side(weight):
        flat_weight = weight.reshape(depth, width)
        pieces = []
        for d in range(parts):
            piece = lax.dot_general(flat[d], flat_weight, first_part, preferred_element_type=jnp.float32)
            keep = in_block[d * slab_cols : (d + 1) * slab_cols]
            pieces.append(jnp.where(keep[:, None], 0.0, piece).astype(jnp.bfloat16))
        others = lax.psum_scatter(jnp.concatenate(pieces, axis=0), "row", scatter_dimension=0, tiled=True)
        own = lax.dot_general(flat_block, flat_weight, first_part, preferred_element_type=jnp.float32)
        diag_term = jnp.sum(diags[:, :, None] * weight.astype(jnp.float32), axis=0)
        return 0.9 * (own + others.astype(jnp.float32)) + 0.1 * diag_term

    starts = [right_side(lax.slice_in_dim(weights, s * width, (s + 1) * width, axis=2)) for s in range(STREAMS)]
    start = jnp.concatenate(starts, axis=1)

    total, diag_slabs = col_gather(col_parts, slabs.reshape(-1, slab_cols), some_diags)
    diag = jnp.sum(diag_slabs.reshape(col_parts, row_count, padded), axis=0)[:, :slab_rows].reshape(-1, 1)

    start = start.reshape(slab_rows, row_count, col_count // row_count).swapaxes(0, 1)
    high = lax.reduce_precision(start, 8, 7)
    low = (start - high).astype(jnp.bfloat16)
    merged, residual = solve(row_count, high.astype(jnp.bfloat16), low, total, diag)

    def placed(array):
        return array.swapaxes(0, 1).reshape(slab_rows, col_count).astype(jnp.float32)

    return placed(merged), placed(residual)


def solution(mesh):
    placed = (P(None, "row", "col"), P(None, "row", "col"))
    return jax.shard_map(
        functools.partial(shards, mesh.shape["row"], mesh.shape["col"]),
        mesh=mesh,
        in_specs=placed,
        out_specs=(P("row", "col"), P("row", "col")),
        check_vma=False,
    )
```

time: 699 us -> 680 us (0.973); the launches traced: 689 us -> 679 us
  waiting for transfers between devices: 263 us -> 81.7 us
  Pallas kernels: 294 us -> 457 us
  local copies, waits for them, and re-layouts: 14.2 us -> 44.1 us
  other arithmetic: 54.8 us -> 32.6 us
    reduce_scatter x2, waiting for transfers between devices: 181 us -> 0.01 us  [right_side(): lax.psum_scatter(jnp.concatenate(pieces, axis=0), 'row', scatter_dimensio...]
    pallas_call x6 -> x3, Pallas kernels: 294 us -> 457 us  [the longest x1 187 us: solve(): pl.pallas_call(functools.partial(solve_kernel, n, parts), out_shape=(out,...]
    convert_element_type x0 -> x4, local copies, waits for them, and re-layouts: none -> 20.7 us  [placed(): array.swapaxes(0, 1).reshape(slab_rows, col_count).astype(jnp.float32)]
    reduce_sum x4 -> x3, other arithmetic: 17.4 us -> 0.76 us  [the longest x1 0.43 us: shards(): own_total = jnp.sum(grams.astype(jnp.float32), axis=0)]
    reshape x0 -> x3, local copies, waits for them, and re-layouts: none -> 7.07 us  [the longest x1 3.61 us: shards(): start.reshape(slab_rows, row_count, col_count // row_count).swapaxes(0, 1)]
  transfers between devices with their start and end apart: 3 -> 3, of which waited for: 3 -> 1; matrix products, arithmetic and copies ran while one was open for 9% -> 8% of each run, Pallas kernels for 0% -> 40%
where the time goes in v1:
time: 680 us; the launch traced here: 679 us
  Pallas kernels  457 us (67%)
  waiting for transfers between devices  81.7 us (12%)
  matrix products  49.5 us (7%)
  local copies, waits for them, and re-layouts  44.1 us (6%)
  other arithmetic  32.6 us (5%)
  between operations  14 us (2%)
    pallas_call x1, Pallas kernels, solve(): pl.pallas_call(functools.partial(solve_kernel, n, parts), out_shape=(out,...  187 us
    pallas_call x1, Pallas kernels, col_gather(): pl.pallas_call(functools.partial(col_gather_kernel, parts, pieces), out_s...  145 us
    pallas_call x1, Pallas kernels, row_gather(): pl.pallas_call(functools.partial(row_gather_kernel, n), out_shape=(shape,...  125 us
    all_gather x1, waiting for transfers between devices, shards(): gathered = lax.all_gather(grams, 'col', axis=0)  81 us
    dot_general x8, matrix products, right_side(): lax.dot_general(flat[d], flat_weight, first_part, preferred_element_type=...  39.6 us
    convert_element_type x4, local copies, waits for them, and re-layouts, placed(): array.swapaxes(0, 1).reshape(slab_rows, col_count).astype(jnp.float32)  20.7 us
  transfers between devices with their start and end apart: 3, of which 1 were waited for; matrix products, arithmetic and copies ran while one was open for 8% of the time, Pallas kernels for 40%

profile of v1, /device:TPU:28, one launch (start us, length us, event | category | flops | bytes accessed | tf_op | source)
XLA Modules:
  0.0 679.3 jit_solution(10912539793499925192)
XLA Ops:
  8.0 5.1 fusion.9
  13.1 81.0 %all-gather.3.cloned.1.call-done = bf16[16,448,896]{2,1,0:T(8,128)(2,1)} async-done(((bf16[4,448,896]{2,1,0:T(8,128)(2,1)}), bf16[16,448,896]{2,1,0:T(8,128)(2,1)}) %all-gather.3.cloned.1.call-update) | async-done | bytes 12845072 | tf_op jit(solution)/shard_map/all_gather | solution.py:338
  94.1 5.7 fusion.8
  99.9 5.2 select_convert_fusion.4
  105.1 4.6 select_convert_fusion.5
  109.7 4.6 select_convert_fusion.6
  114.3 4.7 select_convert_fusion.7
  119.0 6.0 pad_maximum_fusion
  125.3 6.7 select_convert_fusion
  132.0 4.6 select_convert_fusion.1
  136.6 4.6 select_convert_fusion.2
  141.2 4.6 select_convert_fusion.3
  145.8 6.1 pad_maximum_fusion.1
  156.3 125.5 %shard_map.41 = (bf16[8,448,896]{2,1,0:T(8,128)(2,1)}, f32[8,8,128]{2,1,0:T(8,128)}) custom-call(bf16[448,896]{1,0:T(8,128)(2,1)} %fusion.2.x_ref, f32[8,128]{1,0:T(8,128)} %pad_bitcast_fusion.d_ref), custom_call_target="tpu_custom_call" | custom-call | bytes 209715200 | tf_op jit(solution)/shard_map/pallas_call | solution.py:76
  285.4 145.1 %shard_map.42 = (bf16[4,3584,896]{2,1,0:T(8,128)(2,1)}, f32[4,8,8,128]{3,2,1,0:T(8,128)S(1)}) custom-call(bf16[3584,896]{1,0:T(8,128)(2,1)S(1)} %bitcast.45, f32[8,8,128]{2,1,0:T(8,128)S(1)} %copy-done.1), custom_call_target="tpu_custom_call" | custom-call | bytes 419430400 | tf_op jit(solution)/shard_map/pallas_call | solution.py:149
  437.0 5.2 multiply_reduce_fusion.1
  442.3 5.7 multiply_add_fusion.1
  447.9 4.2 multiply_add_fusion
  456.0 5.2 fusion
  461.2 186.6 %shard_map.43 = (bf16[8,448,224]{2,1,0:T(8,128)(2,1)}, bf16[8,448,224]{2,1,0:T(8,128)(2,1)}) custom-call(bf16[8,448,224]{2,1,0:T(8,128)(2,1)} %get-tuple-element.25.hi_ref, bf16[8,448,224]{2,1,0:T(8,128)(2,1)} %get-tuple-element.24.lo_ref, bf16[4,3584,896]{2,1,0:T(8,128)(2,1)} %get-tuple-element.10.t_ref, f32[3584,1]{1,0:T(8,128)} %reshape.80.d_ref), custom_call_target="tpu_custom_call" | custom-call | tf_op jit(solution)/shard_map/pallas_call | solution.py:300
  647.7 4.3 convert_bitcast_fusion
  656.0 5.4 reshape.69
  661.4 6.0 copy.11
  667.4 5.4 reshape.70
  (51 shorter events, 23.2 us)
Async XLA Ops:
  7.2 86.9 %all-gather.3.cloned.1.call-start = ((), (), s32[]{:S(2)}) async-start(), calls=%async_computation.4 | async-start | bytes 16056320 | tf_op jit(solution)/shard_map/all_gather | solution.py:338
  7.9 434.4 %reduce-scatter.3.cloned.1.call-start = ((), (), s32[]{:S(2)}) async-start(), calls=%async_computation.2 | async-start | bytes 7225344 | tf_op jit(solution)/shard_map/reduce_scatter | solution.py:363
  13.1 128.1 %copy-start.2 = (bf16[4,448,896]{2,1,0:T(8,128)(2,1)}, bf16[4,448,896]{2,1,0:T(8,128)(2,1)S(1)}, u32[]{:S(2)}) copy-start(bf16[4,448,896]{2,1,0:T(8,128)(2,1)S(1)} %get-tuple-element.23) | copy-start | bytes 9633796
  94.1 5.8 copy-start.3
  99.8 5.2 copy-start.10
  99.8 9.9 %copy-start.12 = (bf16[4,448,896]{2,1,0:T(8,128)(2,1)}, bf16[4,448,896]{2,1,0:T(8,128)(2,1)S(1)}, u32[]{:S(2)}) copy-start(bf16[4,448,896]{2,1,0:T(8,128)(2,1)S(1)} %get-tuple-element.19) | copy-start | bytes 9633796
  99.8 9.8 %copy-start.8 = (bf16[4,448,896]{2,1,0:T(8,128)(2,1)}, bf16[4,448,896]{2,1,0:T(8,128)(2,1)S(1)}, u32[]{:S(2)}) copy-start(bf16[4,448,896]{2,1,0:T(8,128)(2,1)S(1)} %get-tuple-element.21) | copy-start | bytes 9633796
  99.8 14.4 %copy-start.6 = (bf16[4,448,896]{2,1,0:T(8,128)(2,1)}, bf16[4,448,896]{2,1,0:T(8,128)(2,1)S(1)}, u32[]{:S(2)}) copy-start(bf16[4,448,896]{2,1,0:T(8,128)(2,1)S(1)} %get-tuple-element.18) | copy-start | bytes 9633796
  125.0 322.9 %reduce-scatter.5.cloned.1.call-start = ((), (), s32[]{:S(2)}) async-start(), calls=%async_computation.3 | async-start | bytes 7225344 | tf_op jit(solution)/shard_map/reduce_scatter | solution.py:363
  125.3 6.8 copy-start.11
  132.0 4.6 copy-start.9
  136.6 4.6 copy-start.7
  152.0 1.9 copy-start.4
  281.8 2.9 copy-start
  284.7 0.8 copy-start.1
  447.9 4.2 copy-start.5
Sparse Core Ops, SparseCore 0:
  9.5 84.4 all-gather.2
  125.2 159.8 reduce-scatter.2
  288.7 119.9 reduce-scatter.4

commit v2 on v1

v2 whole, which is shorter than its diff:
```python
import functools

import jax
import jax.numpy as jnp
from jax import lax
from jax.experimental import pallas as pl
from jax.experimental.pallas import tpu as pltpu
from jax.sharding import PartitionSpec as P

ITERS = 2
MESH = pl.DeviceIdType.MESH
VMEM_BYTES = 63 * 2**20


def ring_position(index, n):
    odd = index % 2
    return (1 - odd) * (index // 2) + odd * (n - 1 - index // 2)


def ring_index(position, n):
    back = position // (n // 2)
    return (1 - back) * 2 * position + back * (2 * (n - 1 - position) + 1)


def remote(source, target, send, recv, where):
    return pltpu.make_async_remote_copy(
        src_ref=source, dst_ref=target, send_sem=send, recv_sem=recv, device_id=where, device_id_type=MESH
    )


def reduce_kernel(
    n, parts, gt_ref, w_ref, slab_ref, d_ref, out_ref, t_ref, dt_ref,
    gt, sent, came, part, e_block, dg_out, dg_in, d_ring,
    g_own, g_send, g_recv, r_send, r_recv, t_own, t_send, t_recv, td_send, td_recv,
    x_send, x_recv, f_send, f_recv, dc_send, dc_recv, dg_send, dg_recv,
):
    f32, bf16 = jnp.float32, jnp.bfloat16
    row, col = lax.axis_index("row"), lax.axis_index("col")
    place = ring_position(row, n)
    chips, hops = parts // 2, n // 2
    chip, core = col // 2, col % 2
    rows, slab_cols = slab_ref.shape
    q = w_ref.shape[2]
    span = 2 * slab_cols
    half = span // 2
    cut = rows // 32 * 16
    twin = {"col": chip * 2 + 1 - core}

    def at(distance):
        return ring_index((place + n + distance) % n, n)

    right, left = {"row": at(1)}, {"row": at(-1)}

    def peer(k):
        return {"col": (chip + k) % chips * 2 + core}

    def cols_of(c):
        return pl.ds(pl.multiple_of(c * slab_cols, 16), slab_cols)

    def block(i):
        return pl.ds(pl.multiple_of(i * rows, 16), rows)

    barrier = pltpu.get_barrier_semaphore()
    for k in range(1, n):
        pl.semaphore_signal(barrier, inc=1, device_id={"row": (row + k) % n}, device_id_type=MESH)
    for k in range(1, parts):
        pl.semaphore_signal(barrier, inc=1, device_id={"col": (col + k) % parts}, device_id_type=MESH)
    own_gt = pltpu.make_async_copy(gt_ref, gt.at[cols_of(col), :], g_own)
    own_gt.start()
    own_slab = pltpu.make_async_copy(slab_ref, t_ref.at[col, row], t_own)
    own_slab.start()
    d_ring[row] = d_ref[...]
    zeros = jnp.zeros((half, q), bf16)
    came[0, 0, half:, :] = zeros
    came[1, 0, :half, :] = zeros
    pl.semaphore_wait(barrier, n - 1 + parts - 1)

    def gram_send(k):
        return remote(gt_ref, gt.at[cols_of(col), :], g_send.at[k], g_recv.at[k], peer(k) if k else twin)

    def gram_forward(k):
        origin = gt.at[cols_of((chip + chips - k) % chips * 2 + core), :]
        return remote(origin, origin, g_send.at[chips + k - 1], g_recv.at[chips + k - 1], twin)

    for k in range(chips):
        gram_send(k).start()

    def slab_hop(side, hop, kind):
        owner = at(1 - hop) if side == 0 else at(hop - 1)
        held = t_ref.at[col, owner]
        if kind == "half":
            held = t_ref.at[col, owner, pl.ds(0, cut), :] if side == 0 else t_ref.at[col, owner, pl.ds(cut, rows - cut), :]
        source = slab_ref if kind == "own" else held
        to = left if side else right
        return remote(source, held, t_send.at[side, hop - 1], t_recv.at[side, hop - 1], to)

    def diag_hop(side, hop):
        held = d_ring.at[at(1 - hop) if side == 0 else at(hop - 1)]
        return remote(held, held, td_send.at[side, hop - 1], td_recv.at[side, hop - 1], left if side else right)

    def slab_start(hop, kind):
        for side in range(2):
            slab_hop(side, hop, kind).start()
            if kind != "half" or side == 0:
                diag_hop(side, hop).start()

    def slab_wait(hop, kind):
        for side in range(2):
            slab_hop(side, hop, kind).wait()
            if kind != "half" or side == 0:
                diag_hop(side, hop).wait()

    def item(t):
        return t_ref.at[col, at((1 - 2 * (t % 2)) * ((t + 1) // 2))]

    def item_send(k, t):
        return remote(item(t), item(t), x_send.at[k, t], x_recv.at[k, t], peer(k) if k else twin)

    def item_forward(k, t):
        origin = (chip + chips - k) % chips * 2 + core
        held = t_ref.at[origin, at((1 - 2 * (t % 2)) * ((t + 1) // 2))]
        return remote(held, held, f_send.at[k - 1, t], f_recv.at[k - 1, t], twin)

    def share(t):
        for k in list(range(1, chips)) + [0]:
            item_send(k, t).start()

    def forward(t):
        for k in range(1, chips):
            item_send(k, t).wait_recv()
            item_forward(k, t).start()

    def partial(side, target, base):
        def step(i, carry):
            here = pl.ds(pl.multiple_of(base + i * rows, 16), rows)
            part[side, block(i), :] = jnp.dot(gt[here, :], w_ref[target], preferred_element_type=f32)
            return carry

        lax.fori_loop(0, span // rows, step, 0)

    def ring_hop(phase, side, hop, window):
        return remote(
            sent.at[side, hop - 1, window, :],
            came.at[side, hop - 1, window, :],
            r_send.at[phase, side, hop - 1],
            r_recv.at[phase, side, hop - 1],
            left if side else right,
        )

    halves = (pl.ds(0, half), pl.ds(half, span - half))
    whole = pl.ds(0, span)

    def diag_out(k):
        other = (row + k) % n
        for kind in range(2):
            yield remote(
                dg_out.at[kind, k],
                dg_in.at[kind, block(row), :],
                dg_send.at[kind, k],
                dg_recv.at[kind, k],
                {"row": other},
            )

    def diag_term(target):
        value = jnp.dot(e_block[...], w_ref[target], preferred_element_type=f32)
        high = value.astype(bf16)
        return high, (value - high.astype(f32)).astype(bf16)

    def diag_send(k):
        dg_out[0, k], dg_out[1, k] = diag_term((row + k) % n)
        for copy in diag_out(k):
            copy.start()

    def beside(phase, hop):
        if phase == 0:
            if isinstance(hop, int):
                slab_start(1, "own")
                own_slab.wait()
                share(0)
            else:
                slab_wait(hop - 1, "full")

                @pl.when(hop < hops)
                def _():
                    slab_start(hop, "full")

                @pl.when(hop == hops)
                def _():
                    slab_start(hops, "half")

                share(2 * (hop - 1) - 1)
                share(2 * (hop - 1))
        if phase == chips - 1:
            for k in (2 * hop - 1, 2 * hop):

                @pl.when(k < n)
                def _(k=k):
                    diag_send(k)

            if chips > 1:
                forward(2 * hop - 2)
                forward(2 * hop - 1)

    for phase in range(chips):
        source = (chip + phase) % chips
        base = source * span
        if phase == 0:
            own_gt.wait()
            gram_send(0).wait_recv()
        else:
            gram_send(phase).wait_recv()
            gram_forward(phase).start()
            gram_forward(phase).wait()

        @pl.when(row * rows // span == source)
        def _():
            mine = gt[block(row), :]
            lanes = lax.broadcasted_iota(jnp.int32, mine.shape, 1)
            below = lanes - lax.broadcasted_iota(jnp.int32, mine.shape, 0)
            chosen = below == 0
            for model in range(1, mine.shape[1] // rows):
                chosen = chosen | (below == model * rows)
            e_block[...] = jnp.where(chosen, mine.astype(f32), 0.0).astype(bf16)
            gt[block(row), :] = jnp.where(chosen, 0.0, mine.astype(f32)).astype(bf16)

        partial(0, at(hops), base)
        for side in range(2):
            if phase > 0:
                ring_hop(phase - 1, side, 1, halves[side]).wait_send()
            sent[side, 0, halves[side], :] = part[0, halves[side], :].astype(bf16)
            ring_hop(phase, side, 1, halves[side]).start()
        beside(phase, 1)

        def hop_step(hop, carry, phase=phase, base=base):
            def side_partial(side, carry):
                distance = (1 - 2 * side) * (hops + 1 - hop)
                partial(side, at(distance), base)
                return carry

            lax.fori_loop(0, 2, side_partial, 0)
            for side in range(2):

                @pl.when(hop == 2)
                def _(side=side):
                    ring_hop(phase, side, 1, halves[side]).wait_recv()

                @pl.when(hop > 2)
                def _(side=side):
                    ring_hop(phase, side, hop - 1, whole).wait_recv()

                if phase > 0:
                    ring_hop(phase - 1, side, hop, whole).wait_send()

                def add(i, carry, side=side):
                    value = part[side, block(i), :] + came[side, hop - 2, block(i), :].astype(f32)
                    sent[side, hop - 1, block(i), :] = value.astype(bf16)
                    return carry

                lax.fori_loop(0, span // rows, add, 0)
                ring_hop(phase, side, hop, whole).start()
            beside(phase, hop)
            return carry

        lax.fori_loop(2, hops + 1, hop_step, 0)
        partial(0, row, base)
        for side in range(2):
            ring_hop(phase, side, hops, whole).wait_recv()

        def close(i, carry, base=base):
            value = part[0, block(i), :]
            for side in range(2):
                value += came[side, hops - 1, block(i), :].astype(f32)
            out_ref[pl.ds(pl.multiple_of(base + i * rows, 16), rows), :] = value
            return carry

        lax.fori_loop(0, span // rows, close, 0)
        if phase == 0:
            slab_wait(hops, "half")
            share(n - 1)
            dt_ref[col] = d_ring[...]
            for k in range(1, parts):
                remote(d_ring, dt_ref.at[col], dc_send.at[k], dc_recv.at[k], {"col": (col + k) % parts}).start()

    dg_in[0, block(row), :], dg_in[1, block(row), :] = diag_term(row)

    def diag_wait(k, carry):
        for copy in diag_out(k):
            copy.wait()
        return carry

    lax.fori_loop(1, n, diag_wait, 0)

    def scale(i, carry):
        here = block(i)
        out_ref[here, :] = 0.9 * out_ref[here, :] + (dg_in[0, here, :].astype(f32) + dg_in[1, here, :].astype(f32))
        return carry

    lax.fori_loop(0, n, scale, 0)

    last = chips - 1
    for side in range(2):
        ring_hop(last, side, 1, halves[side]).wait_send()

        def sent_out(hop, carry, side=side):
            ring_hop(last, side, hop, whole).wait_send()
            return carry

        lax.fori_loop(2, hops + 1, sent_out, 0)
    for k in range(chips):
        gram_send(k).wait_send()
    for k in range(1, parts):
        remote(d_ring, dt_ref.at[col], dc_send.at[k], dc_recv.at[k], {"col": (col + k) % parts}).wait()

    def shared(t, carry):
        for k in range(chips):
            item_send(k, t).wait_send()
        item_send(0, t).wait_recv()
        for k in range(1, chips):
            item_forward(k, t).wait()
        return carry

    lax.fori_loop(0, n, shared, 0)


def reduce_columns(n, parts, gt, spread, slab, diag):
    slab_cols, depth = gt.shape
    rows = slab.shape[0]
    q = spread.shape[2]
    hops, chips, span = n // 2, parts // 2, 2 * slab_cols
    f32, bf16 = jnp.float32, jnp.bfloat16
    vmem, any_space = pl.BlockSpec(memory_space=pltpu.VMEM), pl.BlockSpec(memory_space=pl.ANY)
    dma = pltpu.SemaphoreType.DMA
    both = lambda *shape: [dma(shape), dma(shape)]
    return pl.pallas_call(
        functools.partial(reduce_kernel, n, parts),
        out_shape=(
            jax.ShapeDtypeStruct((n * rows, q), f32),
            jax.ShapeDtypeStruct((parts, n, rows, slab_cols), bf16),
            jax.ShapeDtypeStruct((parts, n) + diag.shape, f32),
        ),
        in_specs=[any_space, vmem, vmem, vmem],
        out_specs=(vmem, any_space, vmem),
        scratch_shapes=[
            pltpu.VMEM((parts * slab_cols, depth), bf16),
            pltpu.VMEM((2, hops, span, q), bf16),
            pltpu.VMEM((2, hops, span, q), bf16),
            pltpu.VMEM((2, span, q), f32),
            pltpu.VMEM((rows, depth), bf16),
            pltpu.VMEM((2, n, rows, q), bf16),
            pltpu.VMEM((2, n * rows, q), bf16),
            pltpu.VMEM((n,) + diag.shape, f32),
            dma,
            *both(2 * chips),
            *both(chips, 2, hops),
            dma,
            *both(2, hops),
            *both(2, hops),
            *both(chips, n),
            *both(max(chips - 1, 1), n),
            *both(parts),
            *both(2, n),
        ],
        compiler_params=pltpu.CompilerParams(collective_id=1, has_side_effects=True, vmem_limit_bytes=VMEM_BYTES),
    )(gt, spread, slab, diag)


def solve_kernel(
    n, parts, direction, t_ref, d_ref, om_ref, or_ref,
    tv, v, residual, mapped, out_m, out_r, t_sem, send, recv,
):
    me = lax.axis_index("row")
    rows, q = om_ref.shape[1], om_ref.shape[2]
    depth = tv.shape[2]
    f32 = jnp.float32

    barrier = pltpu.get_barrier_semaphore()
    for k in range(1, n):
        pl.semaphore_signal(barrier, inc=1, device_id={"row": (me + k) % n}, device_id_type=MESH)
    loads = [pltpu.make_async_copy(t_ref.at[c], tv.at[c], t_sem.at[c]) for c in range(parts)]
    for load in loads:
        load.start()

    def block(i):
        return pl.ds(pl.multiple_of(i * rows, 16), rows)

    def product(_):
        def step(i, carry):
            here = block(i)
            total = jnp.zeros((rows, q), f32)
            for c in range(parts):
                total += jnp.dot(tv[c, here, :], v[pl.ds(c * depth, depth), :], preferred_element_type=f32)
            mapped[here, :] = 0.9 * total + d_ref[here, :] * v[here, :].astype(f32)
            return carry

        lax.fori_loop(0, n, step, 0)

    def column_sum(terms):
        def step(i, total):
            return total + jnp.sum(terms(block(i)), axis=0, keepdims=True)

        return lax.fori_loop(0, n, step, jnp.zeros((1, q), f32))

    def first(here):
        start = direction[here, :]
        v[here, :] = start.astype(jnp.bfloat16)
        return start * start

    norm = column_sum(first)
    for load in loads:
        load.wait()
    product(0)
    curvature = column_sum(lambda here: direction[here, :] * mapped[here, :])
    step_a = norm / curvature

    def second(here):
        left = direction[here, :] - step_a * mapped[here, :]
        residual[here, :] = left
        return left * left

    norm_next = column_sum(second)
    scale = norm_next / norm

    def turn(i, carry):
        here = block(i)
        v[here, :] = (residual[here, :] + scale * direction[here, :]).astype(jnp.bfloat16)
        return carry

    lax.fori_loop(0, n, turn, 0)
    product(0)
    curvature = column_sum(lambda here: (residual[here, :] + scale * direction[here, :]) * mapped[here, :])
    step_b = norm_next / curvature

    pl.semaphore_wait(barrier, n - 1)

    def leaving(k):
        i = (me + k) % n
        return [
            remote(held.at[block(i), :], target.at[me], send.at[kind, k], recv.at[kind, k], {"row": i})
            for kind, held, target in ((0, out_m, om_ref), (1, out_r, or_ref))
        ]

    def outputs(i):
        here = block(i)
        left, start = residual[here, :], direction[here, :]
        merged = step_a * start + step_b * (left + scale * start)
        return merged.astype(jnp.bfloat16), (left - step_b * mapped[here, :]).astype(jnp.bfloat16)

    def finish(k, carry):
        i = (me + k) % n
        here = block(i)
        out_m[here, :], out_r[here, :] = outputs(i)

        @pl.when(k > 1)
        def _():
            for copy in leaving(k - 1):
                copy.start()

        return carry

    lax.fori_loop(1, n, finish, 0)
    om_ref[me], or_ref[me] = outputs(me)
    for copy in leaving(n - 1):
        copy.start()

    def drain(k, carry):
        for copy in leaving(k):
            copy.wait()
        return carry

    lax.fori_loop(1, n, drain, 0)


def solve(n, start, total, diag):
    parts = total.shape[0]
    all_rows, q = start.shape
    vmem = pl.BlockSpec(memory_space=pltpu.VMEM)
    half, full = pltpu.VMEM((all_rows, q), jnp.bfloat16), pltpu.VMEM((all_rows, q), jnp.float32)
    out = jax.ShapeDtypeStruct((n, all_rows // n, q), jnp.bfloat16)
    return pl.pallas_call(
        functools.partial(solve_kernel, n, parts),
        out_shape=(out, out),
        in_specs=[vmem, pl.BlockSpec(memory_space=pl.ANY), vmem],
        out_specs=(vmem, vmem),
        scratch_shapes=[
            pltpu.VMEM(total.shape, jnp.bfloat16),
            half,
            full,
            full,
            half,
            half,
            pltpu.SemaphoreType.DMA((parts,)),
            pltpu.SemaphoreType.DMA((2, n)),
            pltpu.SemaphoreType.DMA((2, n)),
        ],
        compiler_params=pltpu.CompilerParams(collective_id=2, has_side_effects=True, vmem_limit_bytes=VMEM_BYTES),
    )(start, total, diag)


def spread_kernel(x_ref, out_ref):
    n, _, q = out_ref.shape
    for j in range(n):
        out_ref[j] = x_ref[:, j * q : (j + 1) * q]


def spread_columns(n, flat):
    rows, columns = flat.shape
    tile = rows // 7 if rows % 112 == 0 else rows
    return pl.pallas_call(
        spread_kernel,
        grid=(rows // tile,),
        out_shape=jax.ShapeDtypeStruct((n, rows, columns // n), flat.dtype),
        in_specs=[pl.BlockSpec((tile, columns), lambda i: (i, 0))],
        out_specs=pl.BlockSpec((n, tile, columns // n), lambda i: (0, i, 0)),
    )(flat)


def join_kernel(a_ref, b_ref, a_out, b_out):
    n, _, q = a_ref.shape
    for source, target in ((a_ref, a_out), (b_ref, b_out)):
        for j in range(n):
            target[:, j * q : (j + 1) * q] = source[j].astype(target.dtype)


def join_columns(a, b):
    n, rows, q = a.shape
    tile = rows // 7 if rows % 112 == 0 else rows
    out = jax.ShapeDtypeStruct((rows, n * q), jnp.float32)
    taken = pl.BlockSpec((n, tile, q), lambda i: (0, i, 0))
    given = pl.BlockSpec((tile, n * q), lambda i: (i, 0))
    return pl.pallas_call(
        join_kernel, grid=(rows // tile,), out_shape=(out, out), in_specs=[taken, taken], out_specs=(given, given)
    )(a, b)


def shards(n, parts, grams, weights):
    models, rows, slab_cols = grams.shape

    own_total = jnp.sum(grams.astype(jnp.float32), axis=0)
    row_ids = lax.axis_index("row") * rows + jnp.arange(rows)[:, None]
    col_ids = lax.axis_index("col") * slab_cols + jnp.arange(slab_cols)[None, :]
    diagonal = row_ids == col_ids
    slab = jnp.where(diagonal, 0.0, own_total).astype(jnp.bfloat16)
    own_diag = jnp.sum(jnp.where(diagonal, own_total, 0.0), axis=1)
    padded = -(-rows // 1024) * 1024
    own_diag = jnp.pad(own_diag, (0, padded - rows)).reshape(-1, 128)

    transposed = grams.transpose(2, 0, 1).reshape(slab_cols, models * rows)
    spread = spread_columns(n, weights.reshape(models * rows, -1))
    start, total, diag_slabs = reduce_columns(n, parts, transposed, spread, slab, own_diag)
    diag = jnp.sum(diag_slabs.reshape(parts, n, padded), axis=0)[:, :rows].reshape(-1, 1)
    merged, residual = solve(n, start, total.reshape(parts, n * rows, slab_cols), diag)
    return join_columns(merged, residual)


def solution(mesh):
    placed = (P(None, "row", "col"), P(None, "row", "col"))
    return jax.shard_map(
        functools.partial(shards, mesh.shape["row"], mesh.shape["col"]),
        mesh=mesh,
        in_specs=placed,
        out_specs=(P("row", "col"), P("row", "col")),
        check_vma=False,
    )
```

time: 680 us -> 455 us (0.67)
  waiting for transfers between devices: 81.7 us -> 0 us
  matrix products: 49.5 us -> 0 us
  local copies, waits for them, and re-layouts: 44.1 us -> 7.25 us
  other arithmetic: 32.6 us -> 4.86 us
  Pallas kernels: 457 us -> 441 us
  between operations: 14 us -> 0.7 us
    all_gather x1 -> x0, waiting for transfers between devices: 81 us -> none  [shards(): gathered = lax.all_gather(grams, 'col', axis=0)]
    pallas_call x1, Pallas kernels: 187 us -> 115 us  [solve(): pl.pallas_call(functools.partial(solve_kernel, n, parts), out_shape=(out,...]
    pallas_call x2 -> x3, Pallas kernels: 271 us -> 327 us  [the longest x1 310 us: reduce_columns(): pl.pallas_call(functools.partial(reduce_kernel, n, parts), out_shape=(jax...]
    dot_general x10 -> x0, matrix products: 49.5 us -> none  [the longest x8 39.6 us: right_side(): lax.dot_general(flat[d], flat_weight, first_part, preferred_element_type=...]
    convert_element_type x4 -> x0, local copies, waits for them, and re-layouts: 20.7 us -> none  [placed(): array.swapaxes(0, 1).reshape(slab_rows, col_count).astype(jnp.float32)]
    concatenate x3 -> x0, other arithmetic: 12.4 us -> none  [the longest x2 12.2 us: right_side(): jnp.concatenate(pieces, axis=0)]
    slice x4 -> x1, local copies, waits for them, and re-layouts: 10.8 us -> 0.01 us  [shards(): jnp.sum(diag_slabs.reshape(parts, n, padded), axis=0)[:, :rows]]
    convert_element_type x2 -> x0, other arithmetic: 9.54 us -> none  [the longest x1 5.21 us: shards(): low = (start - high).astype(jnp.bfloat16)]
  transfers between devices with their start and end apart: 3 -> 0, of which waited for: 1 -> 0; matrix products, arithmetic and copies ran while one was open for 8% -> 0% of each run, Pallas kernels for 40% -> 0%
where the time goes in v2:
time: 455 us; the launch traced here: 454 us
  Pallas kernels  441 us (97%)
  local copies, waits for them, and re-layouts  7.25 us (2%)
  other arithmetic  4.86 us (1%)
    pallas_call x1, Pallas kernels, reduce_columns(): pl.pallas_call(functools.partial(reduce_kernel, n, parts), out_shape=(jax...  310 us
    pallas_call x1, Pallas kernels, solve(): pl.pallas_call(functools.partial(solve_kernel, n, parts), out_shape=(out,...  115 us
    pallas_call x1, Pallas kernels, spread_columns(): pl.pallas_call(spread_kernel, grid=(rows // tile,), out_shape=jax.ShapeDt...  9.5 us

profile of v2, /device:TPU:28, one launch (start us, length us, event | category | flops | bytes accessed | tf_op | source)
XLA Modules:
  0.0 453.9 jit_solution(15181276690332016384)
XLA Ops:
  0.7 2.5 convert_reduce_fusion
  3.2 0.0 copy-start
  3.2 0.3 fusion.1
  3.5 1.1 fusion.slab_ref
  4.6 0.6 pad_bitcast_fusion.d_ref
  5.2 0.2 copy-done
  5.4 3.6 copy.7.gt_ref
  9.0 9.5 %shard_map.41.w_ref = bf16[8,1792,224]{2,1,0:T(8,128)(2,1)} custom-call(bf16[1792,1792]{1,0:T(8,128)(2,1)} %bitcast.13), custom_call_target="tpu_custom_call" | custom-call | tf_op jit(solution)/shard_map/pallas_call | solution.py:508
  18.5 310.3 %shard_map.42 = (f32[3584,224]{1,0:T(8,128)}, bf16[4,8,448,896]{3,2,1,0:T(8,128)(2,1)}, f32[4,8,8,128]{3,2,1,0:T(8,128)}) custom-call(bf16[896,1792]{1,0:T(8,128)(2,1)} %copy.7.gt_ref, bf16[8,1792,224]{2,1,0:T(8,128)(2,1)} %shard_map.41.w_ref, bf16[448,896]{1,0:T(8,128)(2,1)} %fusion.slab_ref, f32[8,128]{1,0:T(8,128)} %pad_bitcast_fusion.d_ref), custom_call_target="tpu_custom_call" | custom-call | tf_op jit(solution)/shard_map/pallas_call | solution.py:334
  328.8 0.9 reduce_sum.31
  329.8 2.8 reshape.36.d_ref
  332.6 114.6 %shard_map.43 = (bf16[8,448,224]{2,1,0:T(8,128)(2,1)}, bf16[8,448,224]{2,1,0:T(8,128)(2,1)}) custom-call(f32[3584,224]{1,0:T(8,128)} %get-tuple-element.7.direction, bf16[4,3584,896]{2,1,0:T(8,128)(2,1)} %bitcast.11, f32[3584,1]{1,0:T(8,128)} %reshape.36.d_ref), custom_call_target="tpu_custom_call" | custom-call | tf_op jit(solution)/shard_map/pallas_call | solution.py:479
  447.2 6.8 %shard_map.44 = (f32[448,1792]{1,0:T(8,128)}, f32[448,1792]{1,0:T(8,128)}) custom-call(bf16[8,448,224]{2,1,0:T(8,128)(2,1)} %get-tuple-element.10.a_ref, bf16[8,448,224]{2,1,0:T(8,128)(2,1)} %get-tuple-element.11.b_ref), custom_call_target="tpu_custom_call" | custom-call | tf_op jit(solution)/shard_map/pallas_call | solution.py:530
  (4 shorter events, 0.0 us)
Async XLA Ops:
  3.2 2.2 copy-start

commit v3 on v2

--- a/solution.py
+++ b/solution.py
@@ -30,9 +30,9 @@
 
 def reduce_kernel(
     n, parts, gt_ref, w_ref, slab_ref, d_ref, out_ref, t_ref, dt_ref,
-    gt, sent, came, part, e_block, dg_out, dg_in, d_ring,
+    gt, sent, came, part, e_block, lo_sent, lo_came, d_ring,
     g_own, g_send, g_recv, r_send, r_recv, t_own, t_send, t_recv, td_send, td_recv,
-    x_send, x_recv, f_send, f_recv, dc_send, dc_recv, dg_send, dg_recv,
+    x_send, x_recv, f_send, f_recv, dc_send, dc_recv, lo_send, lo_recv,
 ):
     f32, bf16 = jnp.float32, jnp.bfloat16
     row, col = lax.axis_index("row"), lax.axis_index("col")
@@ -150,26 +150,29 @@
     halves = (pl.ds(0, half), pl.ds(half, span - half))
     whole = pl.ds(0, span)
 
-    def diag_out(k):
-        other = (row + k) % n
-        for kind in range(2):
-            yield remote(
-                dg_out.at[kind, k],
-                dg_in.at[kind, block(row), :],
-                dg_send.at[kind, k],
-                dg_recv.at[kind, k],
-                {"row": other},
-            )
+    def slot(hop, u):
+        return hop * (hop - 1) // 2 + u
+
+    def low_hop(side, hop, u):
+        here = slot(hop, u)
+        return remote(
+            lo_sent.at[side, here],
+            lo_came.at[side, here],
+            lo_send.at[side, here],
+            lo_recv.at[side, here],
+            left if side else right,
+        )
+
+    def member(side, u):
+        return at((2 * side - 1) * u)
+
+    def carried(side, hop, u, source, shift):
+        first = member(side, u + shift) * rows
+        used = (u < hop - 1) | ((first % span) // half == side)
+        return used if source is None else used & (first // span == source)
 
     def diag_term(target):
-        value = jnp.dot(e_block[...], w_ref[target], preferred_element_type=f32)
-        high = value.astype(bf16)
-        return high, (value - high.astype(f32)).astype(bf16)
-
-    def diag_send(k):
-        dg_out[0, k], dg_out[1, k] = diag_term((row + k) % n)
-        for copy in diag_out(k):
-            copy.start()
+        return jnp.dot(e_block[...], w_ref[target], preferred_element_type=f32) * (1 / 9)
 
     def beside(phase, hop):
         if phase == 0:
@@ -190,16 +193,9 @@
 
                 share(2 * (hop - 1) - 1)
                 share(2 * (hop - 1))
-        if phase == chips - 1:
-            for k in (2 * hop - 1, 2 * hop):
-
-                @pl.when(k < n)
-                def _(k=k):
-                    diag_send(k)
-
-            if chips > 1:
-                forward(2 * hop - 2)
-                forward(2 * hop - 1)
+        if phase == chips - 1 and chips > 1:
+            forward(2 * hop - 2)
+            forward(2 * hop - 1)
 
     for phase in range(chips):
         source = (chip + phase) % chips
@@ -210,7 +206,7 @@
         else:
             gram_send(phase).wait_recv()
             gram_forward(phase).start()
-            gram_forward(phase).wait()
+            gram_forward(phase).wait_recv()
 
         @pl.when(row * rows // span == source)
         def _():
@@ -221,17 +217,26 @@
             for model in range(1, mine.shape[1] // rows):
                 chosen = chosen | (below == model * rows)
             e_block[...] = jnp.where(chosen, mine.astype(f32), 0.0).astype(bf16)
-            gt[block(row), :] = jnp.where(chosen, 0.0, mine.astype(f32)).astype(bf16)
 
         partial(0, at(hops), base)
         for side in range(2):
             if phase > 0:
                 ring_hop(phase - 1, side, 1, halves[side]).wait_send()
             sent[side, 0, halves[side], :] = part[0, halves[side], :].astype(bf16)
+
+            @pl.when(carried(side, 1, 0, source, 0))
+            def _(side=side, base=base):
+                here = pl.ds(pl.multiple_of(row * rows - base, 16), rows)
+                value = part[0, here, :] + diag_term(at(hops))
+                high = value.astype(bf16)
+                sent[side, 0, here, :] = high
+                lo_sent[side, 0] = (value - high.astype(f32)).astype(bf16)
+                low_hop(side, 1, 0).start()
+
             ring_hop(phase, side, 1, halves[side]).start()
         beside(phase, 1)
 
-        def hop_step(hop, carry, phase=phase, base=base):
+        def hop_step(hop, carry, phase=phase, base=base, source=source):
             def side_partial(side, carry):
                 distance = (1 - 2 * side) * (hops + 1 - hop)
                 partial(side, at(distance), base)
@@ -257,6 +262,22 @@
                     return carry
 
                 lax.fori_loop(0, span // rows, add, 0)
+                for u in range(hops):
+
+                    @pl.when((u < hop) & carried(side, hop, u, source, 0))
+                    def _(side=side, u=u):
+                        here = pl.ds(pl.multiple_of(member(side, u) * rows - base, 16), rows)
+                        value = part[side, here, :] + came[side, hop - 2, here, :].astype(f32)
+                        if u == 0:
+                            value += diag_term(at((1 - 2 * side) * (hops + 1 - hop)))
+                        else:
+                            low_hop(side, hop - 1, u - 1).wait_recv()
+                            value += lo_came[side, slot(hop - 1, u - 1)].astype(f32)
+                        high = value.astype(bf16)
+                        sent[side, hop - 1, here, :] = high
+                        lo_sent[side, slot(hop, u)] = (value - high.astype(f32)).astype(bf16)
+                        low_hop(side, hop, u).start()
+
                 ring_hop(phase, side, hop, whole).start()
             beside(phase, hop)
             return carry
@@ -270,10 +291,23 @@
             value = part[0, block(i), :]
             for side in range(2):
                 value += came[side, hops - 1, block(i), :].astype(f32)
-            out_ref[pl.ds(pl.multiple_of(base + i * rows, 16), rows), :] = value
+            out_ref[pl.ds(pl.multiple_of(base + i * rows, 16), rows), :] = 0.9 * value
             return carry
 
         lax.fori_loop(0, span // rows, close, 0)
+
+        @pl.when(row * rows // span == source)
+        def _():
+            out_ref[block(row), :] += 0.9 * diag_term(row)
+
+        for side in range(2):
+            for u in range(hops):
+
+                @pl.when(carried(side, hops, u, source, 1))
+                def _(side=side, u=u):
+                    low_hop(side, hops, u).wait_recv()
+                    out_ref[block(member(side, u + 1)), :] += 0.9 * lo_came[side, slot(hops, u)].astype(f32)
+
         if phase == 0:
             slab_wait(hops, "half")
             share(n - 1)
@@ -281,22 +315,6 @@
             for k in range(1, parts):
                 remote(d_ring, dt_ref.at[col], dc_send.at[k], dc_recv.at[k], {"col": (col + k) % parts}).start()
 
-    dg_in[0, block(row), :], dg_in[1, block(row), :] = diag_term(row)
-
-    def diag_wait(k, carry):
-        for copy in diag_out(k):
-            copy.wait()
-        return carry
-
-    lax.fori_loop(1, n, diag_wait, 0)
-
-    def scale(i, carry):
-        here = block(i)
-        out_ref[here, :] = 0.9 * out_ref[here, :] + (dg_in[0, here, :].astype(f32) + dg_in[1, here, :].astype(f32))
-        return carry
-
-    lax.fori_loop(0, n, scale, 0)
-
     last = chips - 1
     for side in range(2):
         ring_hop(last, side, 1, halves[side]).wait_send()
@@ -306,8 +324,21 @@
             return carry
 
         lax.fori_loop(2, hops + 1, sent_out, 0)
+
+        def low_out(hop, carry, side=side):
+            for u in range(hops):
+
+                @pl.when((u < hop) & carried(side, hop, u, None, 0))
+                def _(u=u):
+                    low_hop(side, hop, u).wait_send()
+
+            return carry
+
+        lax.fori_loop(1, hops + 1, low_out, 0)
     for k in range(chips):
         gram_send(k).wait_send()
+    for k in range(1, chips):
+        gram_forward(k).wait_send()
     for k in range(1, parts):
         remote(d_ring, dt_ref.at[col], dc_send.at[k], dc_recv.at[k], {"col": (col + k) % parts}).wait()
 
@@ -327,6 +358,7 @@
     rows = slab.shape[0]
     q = spread.shape[2]
     hops, chips, span = n // 2, parts // 2, 2 * slab_cols
+    slots = hops * (hops + 1) // 2
     f32, bf16 = jnp.float32, jnp.bfloat16
     vmem, any_space = pl.BlockSpec(memory_space=pltpu.VMEM), pl.BlockSpec(memory_space=pl.ANY)
     dma = pltpu.SemaphoreType.DMA
@@ -346,8 +378,8 @@
             pltpu.VMEM((2, hops, span, q), bf16),
             pltpu.VMEM((2, span, q), f32),
             pltpu.VMEM((rows, depth), bf16),
-            pltpu.VMEM((2, n, rows, q), bf16),
-            pltpu.VMEM((2, n * rows, q), bf16),
+            pltpu.VMEM((2, slots, rows, q), bf16),
+            pltpu.VMEM((2, slots, rows, q), bf16),
             pltpu.VMEM((n,) + diag.shape, f32),
             dma,
             *both(2 * chips),
@@ -358,7 +390,7 @@
             *both(chips, n),
             *both(max(chips - 1, 1), n),
             *both(parts),
-            *both(2, n),
+            *both(2, slots),
         ],
         compiler_params=pltpu.CompilerParams(collective_id=1, has_side_effects=True, vmem_limit_bytes=VMEM_BYTES),
     )(gt, spread, slab, diag)
@@ -370,25 +402,30 @@
 ):
     me = lax.axis_index("row")
     rows, q = om_ref.shape[1], om_ref.shape[2]
-    depth = tv.shape[2]
+    depth = tv.shape[3]
     f32 = jnp.float32
 
     barrier = pltpu.get_barrier_semaphore()
     for k in range(1, n):
         pl.semaphore_signal(barrier, inc=1, device_id={"row": (me + k) % n}, device_id_type=MESH)
-    loads = [pltpu.make_async_copy(t_ref.at[c], tv.at[c], t_sem.at[c]) for c in range(parts)]
-    for load in loads:
-        load.start()
+
+    def load(i):
+        return pltpu.make_async_copy(t_ref.at[:, i], tv.at[i], t_sem.at[i])
+
+    for i in range(n):
+        load(i).start()
 
     def block(i):
         return pl.ds(pl.multiple_of(i * rows, 16), rows)
 
-    def product(_):
+    def product(loading):
         def step(i, carry):
+            if loading:
+                load(i).wait()
             here = block(i)
             total = jnp.zeros((rows, q), f32)
             for c in range(parts):
-                total += jnp.dot(tv[c, here, :], v[pl.ds(c * depth, depth), :], preferred_element_type=f32)
+                total += jnp.dot(tv[i, c], v[pl.ds(c * depth, depth), :], preferred_element_type=f32)
             mapped[here, :] = 0.9 * total + d_ref[here, :] * v[here, :].astype(f32)
             return carry
 
@@ -406,9 +443,7 @@
         return start * start
 
     norm = column_sum(first)
-    for load in loads:
-        load.wait()
-    product(0)
+    product(True)
     curvature = column_sum(lambda here: direction[here, :] * mapped[here, :])
     step_a = norm / curvature
 
@@ -426,7 +461,7 @@
         return carry
 
     lax.fori_loop(0, n, turn, 0)
-    product(0)
+    product(False)
     curvature = column_sum(lambda here: (residual[here, :] + scale * direction[here, :]) * mapped[here, :])
     step_b = norm_next / curvature
 
@@ -482,13 +517,13 @@
         in_specs=[vmem, pl.BlockSpec(memory_space=pl.ANY), vmem],
         out_specs=(vmem, vmem),
         scratch_shapes=[
-            pltpu.VMEM(total.shape, jnp.bfloat16),
+            pltpu.VMEM((n, parts) + total.shape[2:], jnp.bfloat16),
             half,
             full,
             full,
             half,
             half,
-            pltpu.SemaphoreType.DMA((parts,)),
+            pltpu.SemaphoreType.DMA((n,)),
             pltpu.SemaphoreType.DMA((2, n)),
             pltpu.SemaphoreType.DMA((2, n)),
         ],
@@ -548,7 +583,7 @@
     spread = spread_columns(n, weights.reshape(models * rows, -1))
     start, total, diag_slabs = reduce_columns(n, parts, transposed, spread, slab, own_diag)
     diag = jnp.sum(diag_slabs.reshape(parts, n, padded), axis=0)[:, :rows].reshape(-1, 1)
-    merged, residual = solve(n, start, total.reshape(parts, n * rows, slab_cols), diag)
+    merged, residual = solve(n, start, total, diag)
     return join_columns(merged, residual)
 
 

time: 455 us -> 452 us (level)
    pallas_call x1, Pallas kernels: 115 us -> 108 us  [solve(): pl.pallas_call(functools.partial(solve_kernel, n, parts), out_shape=(out,...]
where the time goes in v3:
time: 452 us
  Pallas kernels  439 us (97%)
  local copies, waits for them, and re-layouts  7.25 us (2%)
  other arithmetic  4.86 us (1%)
    pallas_call x1, Pallas kernels, reduce_columns(): pl.pallas_call(functools.partial(reduce_kernel, n, parts), out_shape=(jax...  314 us
    pallas_call x1, Pallas kernels, solve(): pl.pallas_call(functools.partial(solve_kernel, n, parts), out_shape=(out,...  108 us
    pallas_call x1, Pallas kernels, spread_columns(): pl.pallas_call(spread_kernel, grid=(rows // tile,), out_shape=jax.ShapeDt...  9.5 us

profile of v3, /device:TPU:28, one launch (start us, length us, event | category | flops | bytes accessed | tf_op | source)
XLA Modules:
  0.0 451.5 jit_solution(259667628727868313)
XLA Ops:
  0.7 2.5 convert_reduce_fusion
  3.2 0.0 copy-start
  3.2 0.3 fusion.1
  3.5 1.1 fusion.slab_ref
  4.6 0.6 pad_bitcast_fusion.d_ref
  5.2 0.2 copy-done
  5.4 3.6 copy.7.gt_ref
  9.0 9.5 %shard_map.41.w_ref = bf16[8,1792,224]{2,1,0:T(8,128)(2,1)} custom-call(bf16[1792,1792]{1,0:T(8,128)(2,1)} %bitcast.11), custom_call_target="tpu_custom_call" | custom-call | tf_op jit(solution)/shard_map/pallas_call | solution.py:543
  18.5 314.4 %shard_map.42 = (f32[3584,224]{1,0:T(8,128)}, bf16[4,8,448,896]{3,2,1,0:T(8,128)(2,1)}, f32[4,8,8,128]{3,2,1,0:T(8,128)}) custom-call(bf16[896,1792]{1,0:T(8,128)(2,1)} %copy.7.gt_ref, bf16[8,1792,224]{2,1,0:T(8,128)(2,1)} %shard_map.41.w_ref, bf16[448,896]{1,0:T(8,128)(2,1)} %fusion.slab_ref, f32[8,128]{1,0:T(8,128)} %pad_bitcast_fusion.d_ref), custom_call_target="tpu_custom_call" | custom-call | tf_op jit(solution)/shard_map/pallas_call | solution.py:366
  332.9 0.9 reduce_sum.31
  333.9 2.8 reshape.32.d_ref
  336.7 108.0 %shard_map.43 = (bf16[8,448,224]{2,1,0:T(8,128)(2,1)}, bf16[8,448,224]{2,1,0:T(8,128)(2,1)}) custom-call(f32[3584,224]{1,0:T(8,128)} %get-tuple-element.7.direction, bf16[4,8,448,896]{3,2,1,0:T(8,128)(2,1)} %get-tuple-element.8.t_ref, f32[3584,1]{1,0:T(8,128)} %reshape.32.d_ref), custom_call_target="tpu_custom_call" | custom-call | tf_op jit(solution)/shard_map/pallas_call | solution.py:514
  444.8 6.8 %shard_map.44 = (f32[448,1792]{1,0:T(8,128)}, f32[448,1792]{1,0:T(8,128)}) custom-call(bf16[8,448,224]{2,1,0:T(8,128)(2,1)} %get-tuple-element.10.a_ref, bf16[8,448,224]{2,1,0:T(8,128)(2,1)} %get-tuple-element.11.b_ref), custom_call_target="tpu_custom_call" | custom-call | tf_op jit(solution)/shard_map/pallas_call | solution.py:565
  (4 shorter events, 0.0 us)
Async XLA Ops:
  3.2 2.2 copy-start

commit v4 on v3

--- a/solution.py
+++ b/solution.py
@@ -29,9 +29,9 @@
 
 
 def reduce_kernel(
-    n, parts, gt_ref, w_ref, slab_ref, d_ref, out_ref, t_ref, dt_ref,
-    gt, sent, came, part, e_block, lo_sent, lo_came, d_ring,
-    g_own, g_send, g_recv, r_send, r_recv, t_own, t_send, t_recv, td_send, td_recv,
+    n, parts, gt_ref, flat_ref, slab_ref, d_ref, out_ref, t_ref, dt_ref,
+    w_ref, staged, gt, sent, came, part, e_block, lo_sent, lo_came, d_ring,
+    w_sem, g_own, g_send, g_recv, r_send, r_recv, t_own, t_send, t_recv, td_send, td_recv,
     x_send, x_recv, f_send, f_recv, dc_send, dc_recv, lo_send, lo_recv,
 ):
     f32, bf16 = jnp.float32, jnp.bfloat16
@@ -40,7 +40,7 @@
     chips, hops = parts // 2, n // 2
     chip, core = col // 2, col % 2
     rows, slab_cols = slab_ref.shape
-    q = w_ref.shape[2]
+    q = out_ref.shape[1]
     span = 2 * slab_cols
     half = span // 2
     cut = rows // 32 * 16
@@ -71,8 +71,9 @@
     own_slab.start()
     d_ring[row] = d_ref[...]
     zeros = jnp.zeros((half, q), bf16)
-    came[0, 0, half:, :] = zeros
-    came[1, 0, :half, :] = zeros
+    for k in range(chips):
+        came[0, 0, k, half:, :] = zeros
+        came[1, 0, k, :half, :] = zeros
     pl.semaphore_wait(barrier, n - 1 + parts - 1)
 
     def gram_send(k):
@@ -138,12 +139,13 @@
 
         lax.fori_loop(0, span // rows, step, 0)
 
-    def ring_hop(phase, side, hop, window):
+    def ring_hop(k, side, hop, window):
+        slot_of = (hop - 1) % 2
         return remote(
-            sent.at[side, hop - 1, window, :],
-            came.at[side, hop - 1, window, :],
-            r_send.at[phase, side, hop - 1],
-            r_recv.at[phase, side, hop - 1],
+            sent.at[side, slot_of, k, window, :],
+            came.at[side, slot_of, k, window, :],
+            r_send.at[k, side, hop - 1],
+            r_recv.at[k, side, hop - 1],
             left if side else right,
         )
 
@@ -174,41 +176,11 @@
     def diag_term(target):
         return jnp.dot(e_block[...], w_ref[target], preferred_element_type=f32) * (1 / 9)
 
-    def beside(phase, hop):
-        if phase == 0:
-            if isinstance(hop, int):
-                slab_start(1, "own")
-                own_slab.wait()
-                share(0)
-            else:
-                slab_wait(hop - 1, "full")
-
-                @pl.when(hop < hops)
-                def _():
-                    slab_start(hop, "full")
-
-                @pl.when(hop == hops)
-                def _():
-                    slab_start(hops, "half")
-
-                share(2 * (hop - 1) - 1)
-                share(2 * (hop - 1))
-        if phase == chips - 1 and chips > 1:
-            forward(2 * hop - 2)
-            forward(2 * hop - 1)
-
-    for phase in range(chips):
-        source = (chip + phase) % chips
-        base = source * span
-        if phase == 0:
-            own_gt.wait()
-            gram_send(0).wait_recv()
-        else:
-            gram_send(phase).wait_recv()
-            gram_forward(phase).start()
-            gram_forward(phase).wait_recv()
-
-        @pl.when(row * rows // span == source)
+    def source_of(k):
+        return (chip + k) % chips
+
+    def extract(k):
+        @pl.when(row * rows // span == source_of(k))
         def _():
             mine = gt[block(row), :]
             lanes = lax.broadcasted_iota(jnp.int32, mine.shape, 1)
@@ -218,80 +190,96 @@
                 chosen = chosen | (below == model * rows)
             e_block[...] = jnp.where(chosen, mine.astype(f32), 0.0).astype(bf16)
 
-        partial(0, at(hops), base)
-        for side in range(2):
-            if phase > 0:
-                ring_hop(phase - 1, side, 1, halves[side]).wait_send()
-            sent[side, 0, halves[side], :] = part[0, halves[side], :].astype(bf16)
-
-            @pl.when(carried(side, 1, 0, source, 0))
-            def _(side=side, base=base):
-                here = pl.ds(pl.multiple_of(row * rows - base, 16), rows)
-                value = part[0, here, :] + diag_term(at(hops))
-                high = value.astype(bf16)
-                sent[side, 0, here, :] = high
-                lo_sent[side, 0] = (value - high.astype(f32)).astype(bf16)
+    def split(k, side, hop, u, value):
+        here = pl.ds(pl.multiple_of(member(side, u) * rows - source_of(k) * span, 16), rows)
+        high = value.astype(bf16)
+        sent[side, (hop - 1) % 2, k, here, :] = high
+        lo_sent[side, slot(hop, u)] = (value - high.astype(f32)).astype(bf16)
+
+    def local(k, side, u):
+        return pl.ds(pl.multiple_of(member(side, u) * rows - source_of(k) * span, 16), rows)
+
+    def first_hop(k):
+        extract(k)
+        partial(0, at(hops), source_of(k) * span)
+        for side in range(2):
+            sent[side, 0, k, halves[side], :] = part[0, halves[side], :].astype(bf16)
+
+            @pl.when(carried(side, 1, 0, source_of(k), 0))
+            def _(side=side):
+                split(k, side, 1, 0, part[0, local(k, side, 0), :] + diag_term(at(hops)))
+
+        for side in range(2):
+            ring_hop(k, side, 1, halves[side]).start()
+
+            @pl.when(carried(side, 1, 0, source_of(k), 0))
+            def _(side=side):
                 low_hop(side, 1, 0).start()
 
-            ring_hop(phase, side, 1, halves[side]).start()
-        beside(phase, 1)
-
-        def hop_step(hop, carry, phase=phase, base=base, source=source):
-            def side_partial(side, carry):
-                distance = (1 - 2 * side) * (hops + 1 - hop)
-                partial(side, at(distance), base)
+    def later_hop(k, hop):
+        source = source_of(k)
+
+        def side_partial(side, carry):
+            partial(side, at((1 - 2 * side) * (hops + 1 - hop)), source * span)
+            return carry
+
+        lax.fori_loop(0, 2, side_partial, 0)
+        for side in range(2):
+
+            @pl.when(hop == 2)
+            def _(side=side):
+                ring_hop(k, side, 1, halves[side]).wait_recv()
+
+            @pl.when(hop > 2)
+            def _(side=side):
+                ring_hop(k, side, hop - 1, whole).wait_recv()
+
+            @pl.when(hop == 3)
+            def _(side=side):
+                ring_hop(k, side, 1, halves[side]).wait_send()
+
+            @pl.when(hop > 3)
+            def _(side=side):
+                ring_hop(k, side, hop - 2, whole).wait_send()
+
+            def add(i, carry, side=side):
+                value = part[side, block(i), :] + came[side, hop % 2, k, block(i), :].astype(f32)
+                sent[side, (hop - 1) % 2, k, block(i), :] = value.astype(bf16)
                 return carry
 
-            lax.fori_loop(0, 2, side_partial, 0)
-            for side in range(2):
-
-                @pl.when(hop == 2)
-                def _(side=side):
-                    ring_hop(phase, side, 1, halves[side]).wait_recv()
-
-                @pl.when(hop > 2)
-                def _(side=side):
-                    ring_hop(phase, side, hop - 1, whole).wait_recv()
-
-                if phase > 0:
-                    ring_hop(phase - 1, side, hop, whole).wait_send()
-
-                def add(i, carry, side=side):
-                    value = part[side, block(i), :] + came[side, hop - 2, block(i), :].astype(f32)
-                    sent[side, hop - 1, block(i), :] = value.astype(bf16)
-                    return carry
-
-                lax.fori_loop(0, span // rows, add, 0)
-                for u in range(hops):
-
-                    @pl.when((u < hop) & carried(side, hop, u, source, 0))
-                    def _(side=side, u=u):
-                        here = pl.ds(pl.multiple_of(member(side, u) * rows - base, 16), rows)
-                        value = part[side, here, :] + came[side, hop - 2, here, :].astype(f32)
-                        if u == 0:
-                            value += diag_term(at((1 - 2 * side) * (hops + 1 - hop)))
-                        else:
-                            low_hop(side, hop - 1, u - 1).wait_recv()
-                            value += lo_came[side, slot(hop - 1, u - 1)].astype(f32)
-                        high = value.astype(bf16)
-                        sent[side, hop - 1, here, :] = high
-                        lo_sent[side, slot(hop, u)] = (value - high.astype(f32)).astype(bf16)
-                        low_hop(side, hop, u).start()
-
-                ring_hop(phase, side, hop, whole).start()
-            beside(phase, hop)
-            return carry
-
-        lax.fori_loop(2, hops + 1, hop_step, 0)
-        partial(0, row, base)
-        for side in range(2):
-            ring_hop(phase, side, hops, whole).wait_recv()
-
-        def close(i, carry, base=base):
+            lax.fori_loop(0, span // rows, add, 0)
+            for u in range(hops):
+
+                @pl.when((u < hop) & carried(side, hop, u, source, 0))
+                def _(side=side, u=u):
+                    here = local(k, side, u)
+                    value = part[side, here, :] + came[side, hop % 2, k, here, :].astype(f32)
+                    if u == 0:
+                        value += diag_term(at((1 - 2 * side) * (hops + 1 - hop)))
+                    else:
+                        low_hop(side, hop - 1, u - 1).wait_recv()
+                        value += lo_came[side, slot(hop - 1, u - 1)].astype(f32)
+                    split(k, side, hop, u, value)
+
+        for side in range(2):
+            ring_hop(k, side, hop, whole).start()
+            for u in range(hops):
+
+                @pl.when((u < hop) & carried(side, hop, u, source, 0))
+                def _(side=side, u=u):
+                    low_hop(side, hop, u).start()
+
+    def close_part(k):
+        source = source_of(k)
+        partial(0, row, source * span)
+        for side in range(2):
+            ring_hop(k, side, hops, whole).wait_recv()
+
+        def close(i, carry):
             value = part[0, block(i), :]
             for side in range(2):
-                value += came[side, hops - 1, block(i), :].astype(f32)
-            out_ref[pl.ds(pl.multiple_of(base + i * rows, 16), rows), :] = 0.9 * value
+                value += came[side, (hops - 1) % 2, k, block(i), :].astype(f32)
+            out_ref[pl.ds(pl.multiple_of(source * span + i * rows, 16), rows), :] = 0.9 * value
             return carry
 
         lax.fori_loop(0, span // rows, close, 0)
@@ -308,22 +296,83 @@
                     low_hop(side, hops, u).wait_recv()
                     out_ref[block(member(side, u + 1)), :] += 0.9 * lo_came[side, slot(hops, u)].astype(f32)
 
-        if phase == 0:
-            slab_wait(hops, "half")
-            share(n - 1)
-            dt_ref[col] = d_ring[...]
-            for k in range(1, parts):
-                remote(d_ring, dt_ref.at[col], dc_send.at[k], dc_recv.at[k], {"col": (col + k) % parts}).start()
-
-    last = chips - 1
+    tile = staged.shape[1]
+    tiles = w_ref.shape[1] // tile
+
+    def staging(i):
+        source = flat_ref.at[pl.ds(pl.multiple_of(i * tile, 16), tile), :]
+        return pltpu.make_async_copy(source, staged.at[i % 2], w_sem.at[i % 2])
+
+    def spread(i, carry):
+        @pl.when(i + 1 < tiles)
+        def _():
+            staging(i + 1).start()
+
+        staging(i).wait()
+        for j in range(n):
+            w_ref[j, pl.ds(pl.multiple_of(i * tile, 16), tile), :] = staged[i % 2, :, j * q : (j + 1) * q]
+        return carry
+
+    slab_start(1, "own")
+    staging(0).start()
+    own_slab.wait()
+    share(0)
+    lax.fori_loop(0, tiles, spread, 0)
+    own_gt.wait()
+    gram_send(0).wait_recv()
+    first_hop(0)
+
+    def slab_step(hop, carry):
+        slab_wait(hop - 1, "full")
+        slab_start(hop, "full")
+        share(2 * (hop - 1) - 1)
+        share(2 * (hop - 1))
+        return carry
+
+    slab_step(2, 0)
+    later_hop(0, jnp.int32(2))
+    lax.fori_loop(3, hops, slab_step, 0)
+    slab_wait(hops - 1, "full")
+    slab_start(hops, "half")
+    share(n - 3)
+    share(n - 2)
+    for k in range(1, chips):
+        gram_send(k).wait_recv()
+        gram_forward(k).start()
+    for k in range(1, chips):
+        gram_forward(k).wait_recv()
+        first_hop(k)
+    slab_wait(hops, "half")
+    share(n - 1)
+    dt_ref[col] = d_ring[...]
+    for k in range(1, parts):
+        remote(d_ring, dt_ref.at[col], dc_send.at[k], dc_recv.at[k], {"col": (col + k) % parts}).start()
+
+    def hop_step(hop, carry):
+        later_hop(0, hop + 1)
+        for k in range(1, chips):
+            later_hop(k, hop)
+        if chips > 1:
+            forward(2 * hop - 4)
+            forward(2 * hop - 3)
+        return carry
+
+    lax.fori_loop(2, hops, hop_step, 0)
+    for k in range(1, chips):
+        later_hop(k, jnp.int32(hops))
+    if chips > 1:
+        forward(n - 4)
+        forward(n - 3)
+    for k in range(chips):
+        close_part(k)
+    if chips > 1:
+        forward(n - 2)
+        forward(n - 1)
+
     for side in range(2):
-        ring_hop(last, side, 1, halves[side]).wait_send()
-
-        def sent_out(hop, carry, side=side):
-            ring_hop(last, side, hop, whole).wait_send()
-            return carry
-
-        lax.fori_loop(2, hops + 1, sent_out, 0)
+        for k in range(chips):
+            ring_hop(k, side, hops - 1, whole if hops > 2 else halves[side]).wait_send()
+            ring_hop(k, side, hops, whole).wait_send()
 
         def low_out(hop, carry, side=side):
             for u in range(hops):
@@ -353,10 +402,11 @@
     lax.fori_loop(0, n, shared, 0)
 
 
-def reduce_columns(n, parts, gt, spread, slab, diag):
+def reduce_columns(n, parts, gt, flat, slab, diag):
     slab_cols, depth = gt.shape
     rows = slab.shape[0]
-    q = spread.shape[2]
+    q = flat.shape[1] // n
+    tile = depth // 7 if depth % 112 == 0 else depth
     hops, chips, span = n // 2, parts // 2, 2 * slab_cols
     slots = hops * (hops + 1) // 2
     f32, bf16 = jnp.float32, jnp.bfloat16
@@ -370,17 +420,20 @@
             jax.ShapeDtypeStruct((parts, n, rows, slab_cols), bf16),
             jax.ShapeDtypeStruct((parts, n) + diag.shape, f32),
         ),
-        in_specs=[any_space, vmem, vmem, vmem],
+        in_specs=[any_space, any_space, vmem, vmem],
         out_specs=(vmem, any_space, vmem),
         scratch_shapes=[
+            pltpu.VMEM((n, depth, q), bf16),
+            pltpu.VMEM((2, tile, n * q), bf16),
             pltpu.VMEM((parts * slab_cols, depth), bf16),
-            pltpu.VMEM((2, hops, span, q), bf16),
-            pltpu.VMEM((2, hops, span, q), bf16),
+            pltpu.VMEM((2, 2, chips, span, q), bf16),
+            pltpu.VMEM((2, 2, chips, span, q), bf16),
             pltpu.VMEM((2, span, q), f32),
             pltpu.VMEM((rows, depth), bf16),
             pltpu.VMEM((2, slots, rows, q), bf16),
             pltpu.VMEM((2, slots, rows, q), bf16),
             pltpu.VMEM((n,) + diag.shape, f32),
+            dma((2,)),
             dma,
             *both(2 * chips),
             *both(chips, 2, hops),
@@ -393,12 +446,12 @@
             *both(2, slots),
         ],
         compiler_params=pltpu.CompilerParams(collective_id=1, has_side_effects=True, vmem_limit_bytes=VMEM_BYTES),
-    )(gt, spread, slab, diag)
+    )(gt, flat, slab, diag)
 
 
 def solve_kernel(
-    n, parts, direction, t_ref, d_ref, om_ref, or_ref,
-    tv, v, residual, mapped, out_m, out_r, t_sem, send, recv,
+    n, parts, direction, t_ref, dt_ref, om_ref, or_ref,
+    tv, d_ref, v, residual, mapped, out_m, out_r, t_sem, send, recv,
 ):
     me = lax.axis_index("row")
     rows, q = om_ref.shape[1], om_ref.shape[2]
@@ -418,7 +471,19 @@
     def block(i):
         return pl.ds(pl.multiple_of(i * rows, 16), rows)
 
-    def product(loading):
+    for i in range(n):
+        lines = dt_ref[0, i]
+        for c in range(1, parts):
+            lines += dt_ref[c, i]
+        for line in range(pl.cdiv(rows, 128)):
+            size = min(128, rows - line * 128)
+            square = jnp.broadcast_to(lines[line : line + 1, :], (size, 128))
+            lanes = lax.broadcasted_iota(jnp.int32, square.shape, 1)
+            chosen = lanes == lax.broadcasted_iota(jnp.int32, square.shape, 0)
+            value = jnp.sum(jnp.where(chosen, square, 0.0), axis=1, keepdims=True)
+            d_ref[pl.ds(i * rows + line * 128, size), :] = value
+
+    def product(loading, toward):
         def step(i, carry):
             if loading:
                 load(i).wait()
@@ -426,10 +491,11 @@
             total = jnp.zeros((rows, q), f32)
             for c in range(parts):
                 total += jnp.dot(tv[i, c], v[pl.ds(c * depth, depth), :], preferred_element_type=f32)
-            mapped[here, :] = 0.9 * total + d_ref[here, :] * v[here, :].astype(f32)
-            return carry
-
-        lax.fori_loop(0, n, step, 0)
+            result = 0.9 * total + d_ref[here, :] * v[here, :].astype(f32)
+            mapped[here, :] = result
+            return carry + jnp.sum(toward(here) * result, axis=0, keepdims=True)
+
+        return lax.fori_loop(0, n, step, jnp.zeros((1, q), f32))
 
     def column_sum(terms):
         def step(i, total):
@@ -443,8 +509,7 @@
         return start * start
 
     norm = column_sum(first)
-    product(True)
-    curvature = column_sum(lambda here: direction[here, :] * mapped[here, :])
+    curvature = product(True, lambda here: direction[here, :])
     step_a = norm / curvature
 
     def second(here):
@@ -461,8 +526,7 @@
         return carry
 
     lax.fori_loop(0, n, turn, 0)
-    product(False)
-    curvature = column_sum(lambda here: (residual[here, :] + scale * direction[here, :]) * mapped[here, :])
+    curvature = product(False, lambda here: residual[here, :] + scale * direction[here, :])
     step_b = norm_next / curvature
 
     pl.semaphore_wait(barrier, n - 1)
@@ -518,6 +582,7 @@
         out_specs=(vmem, vmem),
         scratch_shapes=[
             pltpu.VMEM((n, parts) + total.shape[2:], jnp.bfloat16),
+            pltpu.VMEM((all_rows, 1), jnp.float32),
             half,
             full,
             full,
@@ -531,24 +596,6 @@
     )(start, total, diag)
 
 
-def spread_kernel(x_ref, out_ref):
-    n, _, q = out_ref.shape
-    for j in range(n):
-        out_ref[j] = x_ref[:, j * q : (j + 1) * q]
-
-
-def spread_columns(n, flat):
-    rows, columns = flat.shape
-    tile = rows // 7 if rows % 112 == 0 else rows
-    return pl.pallas_call(
-        spread_kernel,
-        grid=(rows // tile,),
-        out_shape=jax.ShapeDtypeStruct((n, rows, columns // n), flat.dtype),
-        in_specs=[pl.BlockSpec((tile, columns), lambda i: (i, 0))],
-        out_specs=pl.BlockSpec((n, tile, columns // n), lambda i: (0, i, 0)),
-    )(flat)
-
-
 def join_kernel(a_ref, b_ref, a_out, b_out):
     n, _, q = a_ref.shape
     for source, target in ((a_ref, a_out), (b_ref, b_out)):
@@ -580,10 +627,9 @@
     own_diag = jnp.pad(own_diag, (0, padded - rows)).reshape(-1, 128)
 
     transposed = grams.transpose(2, 0, 1).reshape(slab_cols, models * rows)
-    spread = spread_columns(n, weights.reshape(models * rows, -1))
-    start, total, diag_slabs = reduce_columns(n, parts, transposed, spread, slab, own_diag)
-    diag = jnp.sum(diag_slabs.reshape(parts, n, padded), axis=0)[:, :rows].reshape(-1, 1)
-    merged, residual = solve(n, start, total, diag)
+    flat = weights.reshape(models * rows, -1)
+    start, total, diags = reduce_columns(n, parts, transposed, flat, slab, own_diag)
+    merged, residual = solve(n, start, total, diags)
     return join_columns(merged, residual)
 
 

time: 452 us -> 405 us (0.90)
  Pallas kernels: 439 us -> 396 us
    pallas_call x1, Pallas kernels: 314 us -> 276 us  [reduce_columns(): pl.pallas_call(functools.partial(reduce_kernel, n, parts), out_shape=(jax...]
    pallas_call x1 -> x0, Pallas kernels: 9.5 us -> none  [spread_columns(): pl.pallas_call(spread_kernel, grid=(rows // tile,), out_shape=jax.ShapeDt...]
    pallas_call x1, Pallas kernels: 108 us -> 113 us  [solve(): pl.pallas_call(functools.partial(solve_kernel, n, parts), out_shape=(out,...]
where the time goes in v4:
time: 405 us
  Pallas kernels  396 us (98%)
  local copies, waits for them, and re-layouts  4.4 us (1%)
    pallas_call x1, Pallas kernels, reduce_columns(): pl.pallas_call(functools.partial(reduce_kernel, n, parts), out_shape=(jax...  276 us
    pallas_call x1, Pallas kernels, solve(): pl.pallas_call(functools.partial(solve_kernel, n, parts), out_shape=(out,...  113 us

profile of v4, /device:TPU:28, one launch (start us, length us, event | category | flops | bytes accessed | tf_op | source)
XLA Modules:
  0.0 404.5 jit_solution(17409301039970391470)
XLA Ops:
  0.7 2.5 convert_reduce_fusion
  3.2 0.0 copy-start
  3.2 0.3 fusion.1
  3.5 1.1 fusion.slab_ref
  4.6 0.6 pad_bitcast_fusion.d_ref
  5.2 0.2 copy-done
  5.4 3.6 copy.5.gt_ref
  9.0 275.6 %shard_map.41 = (f32[3584,224]{1,0:T(8,128)}, bf16[4,8,448,896]{3,2,1,0:T(8,128)(2,1)}, f32[4,8,8,128]{3,2,1,0:T(8,128)}) custom-call(bf16[896,1792]{1,0:T(8,128)(2,1)} %copy.5.gt_ref, bf16[1792,1792]{1,0:T(8,128)(2,1)} %bitcast.7, bf16[448,896]{1,0:T(8,128)(2,1)} %fusion.slab_ref, f32[8,128]{1,0:T(8,128)} %pad_bitcast_fusion.d_ref), custom_call_target="tpu_custom_call" | custom-call | tf_op jit(solution)/shard_map/pallas_call | solution.py:416
  284.6 113.2 %shard_map.42 = (bf16[8,448,224]{2,1,0:T(8,128)(2,1)}, bf16[8,448,224]{2,1,0:T(8,128)(2,1)}) custom-call(f32[3584,224]{1,0:T(8,128)} %get-tuple-element.7.direction, bf16[4,8,448,896]{3,2,1,0:T(8,128)(2,1)} %get-tuple-element.8.t_ref, f32[4,8,8,128]{3,2,1,0:T(8,128)} %get-tuple-element.9.dt_ref), custom_call_target="tpu_custom_call" | custom-call | tf_op jit(solution)/shard_map/pallas_call | solution.py:578
  397.8 6.8 %shard_map.43 = (f32[448,1792]{1,0:T(8,128)}, f32[448,1792]{1,0:T(8,128)}) custom-call(bf16[8,448,224]{2,1,0:T(8,128)(2,1)} %get-tuple-element.10.a_ref, bf16[8,448,224]{2,1,0:T(8,128)(2,1)} %get-tuple-element.11.b_ref), custom_call_target="tpu_custom_call" | custom-call | tf_op jit(solution)/shard_map/pallas_call | solution.py:612
  (2 shorter events, 0.0 us)
Async XLA Ops:
  3.2 2.2 copy-start

commit v5 on v4

--- a/solution.py
+++ b/solution.py
@@ -329,9 +329,7 @@
         share(2 * (hop - 1))
         return carry
 
-    slab_step(2, 0)
-    later_hop(0, jnp.int32(2))
-    lax.fori_loop(3, hops, slab_step, 0)
+    lax.fori_loop(2, hops, slab_step, 0)
     slab_wait(hops - 1, "full")
     slab_start(hops, "half")
     share(n - 3)
@@ -349,20 +347,14 @@
         remote(d_ring, dt_ref.at[col], dc_send.at[k], dc_recv.at[k], {"col": (col + k) % parts}).start()
 
     def hop_step(hop, carry):
-        later_hop(0, hop + 1)
-        for k in range(1, chips):
+        for k in range(chips):
             later_hop(k, hop)
         if chips > 1:
             forward(2 * hop - 4)
             forward(2 * hop - 3)
         return carry
 
-    lax.fori_loop(2, hops, hop_step, 0)
-    for k in range(1, chips):
-        later_hop(k, jnp.int32(hops))
-    if chips > 1:
-        forward(n - 4)
-        forward(n - 3)
+    lax.fori_loop(2, hops + 1, hop_step, 0)
     for k in range(chips):
         close_part(k)
     if chips > 1:

time: 405 us -> 387 us (0.956); the launches traced: 405 us -> 382 us
  Pallas kernels: 396 us -> 373 us
    pallas_call x1, Pallas kernels: 276 us -> 257 us  [reduce_columns(): pl.pallas_call(functools.partial(reduce_kernel, n, parts), out_shape=(jax...]
where the time goes in v5:
time: 387 us; the launch traced here: 382 us
  Pallas kernels  373 us (96%)
  local copies, waits for them, and re-layouts  4.4 us (1%)
  other arithmetic  3.94 us (1%)
    pallas_call x1, Pallas kernels, reduce_columns(): pl.pallas_call(functools.partial(reduce_kernel, n, parts), out_shape=(jax...  257 us
    pallas_call x1, Pallas kernels, solve(): pl.pallas_call(functools.partial(solve_kernel, n, parts), out_shape=(out,...  110 us

profile of v5, /device:TPU:28, one launch (start us, length us, event | category | flops | bytes accessed | tf_op | source)
XLA Modules:
  0.0 382.1 jit_solution(10806714217392381426)
XLA Ops:
  0.7 2.5 convert_reduce_fusion
  3.2 0.0 copy-start
  3.2 0.3 fusion.1
  3.5 1.1 fusion.slab_ref
  4.6 0.6 pad_bitcast_fusion.d_ref
  5.2 0.2 copy-done
  5.4 3.6 copy.5.gt_ref
  9.0 256.8 %shard_map.41 = (f32[3584,224]{1,0:T(8,128)}, bf16[4,8,448,896]{3,2,1,0:T(8,128)(2,1)}, f32[4,8,8,128]{3,2,1,0:T(8,128)}) custom-call(bf16[896,1792]{1,0:T(8,128)(2,1)} %copy.5.gt_ref, bf16[1792,1792]{1,0:T(8,128)(2,1)} %bitcast.7, bf16[448,896]{1,0:T(8,128)(2,1)} %fusion.slab_ref, f32[8,128]{1,0:T(8,128)} %pad_bitcast_fusion.d_ref), custom_call_target="tpu_custom_call" | custom-call | tf_op jit(solution)/shard_map/pallas_call | solution.py:408
  265.8 109.5 %shard_map.42 = (bf16[8,448,224]{2,1,0:T(8,128)(2,1)}, bf16[8,448,224]{2,1,0:T(8,128)(2,1)}) custom-call(f32[3584,224]{1,0:T(8,128)} %get-tuple-element.7.direction, bf16[4,8,448,896]{3,2,1,0:T(8,128)(2,1)} %get-tuple-element.8.t_ref, f32[4,8,8,128]{3,2,1,0:T(8,128)} %get-tuple-element.9.dt_ref), custom_call_target="tpu_custom_call" | custom-call | tf_op jit(solution)/shard_map/pallas_call | solution.py:570
  375.4 6.8 %shard_map.43 = (f32[448,1792]{1,0:T(8,128)}, f32[448,1792]{1,0:T(8,128)}) custom-call(bf16[8,448,224]{2,1,0:T(8,128)(2,1)} %get-tuple-element.10.a_ref, bf16[8,448,224]{2,1,0:T(8,128)(2,1)} %get-tuple-element.11.b_ref), custom_call_target="tpu_custom_call" | custom-call | tf_op jit(solution)/shard_map/pallas_call | solution.py:604
  (2 shorter events, 0.0 us)
Async XLA Ops:
  3.2 2.2 copy-start
